TPU v7x, 128 devices: a whole 4x4x4 slice. The times are simulated.
128 devices in a mesh: day: 16 (over x_lo, y, core), year: 8 (over z, x_hi).
Axes of the slice: x: 4 (x_hi: 2, x_lo: 2; x = x_hi * 2 + x_lo), y: 4, z: 4, core: 2. Of those that a mesh axis runs over, the one named last changes fastest.
Arguments:
- field: bfloat16 [32, 368, 2, 11520], P('year', 'day'), may hold values from -14 to 14
- day_index: int32 [32, 368], P('year', 'day'), may hold values from 0 to 367, as said below
- sample_count: int32 [32, 368, 2], P('year', 'day'), may hold values from 1 to 4
Outputs:
- anomaly: bfloat16 [32, 368, 2, 11520], P('year', 'day')
- climatology: bfloat16 [368, 2, 11520], P('day', None, 'year')
Inputs may be any that keep to these rules, and one draw needn't show every extreme that they name: In each year either day_index[y, s] = s for every slot, or there is a slot from which on day_index[y, s] = (s + 1) mod 368 and before which day_index[y, s] = s.
All inputs are finite; a program needn't handle non-finite values.
Results may differ from a plain program's by a relative error of at most 0.001.
Values sent between devices are 32-bit elements; how exact they have to be, the bound alone decides.
A program may use at most 128 MiB of HBM per device.

v0:
```python
import jax
import jax.numpy as jnp
from jax import lax
from jax.sharding import PartitionSpec as P

HALF = 30


def passed_along(value, axis, steps):
    count = lax.axis_size(axis)
    pairs = [(source, (source + steps) % count) for source in range(count)]
    return lax.ppermute(value, axis, pairs)


def in_blocks(shard, dim, devices):
    shape = shard.shape
    tiles = shard.reshape(*shape[:dim], devices, shape[dim] // devices, *shape[dim + 1 :])
    return jnp.moveaxis(tiles, dim, 0)


def sent_and_summed(shard, axis, dim):
    devices = lax.axis_size(axis)
    tiles = lax.all_to_all(in_blocks(shard, dim, devices), axis, 0, 0, tiled=True)
    return jnp.sum(tiles, axis=0)


def copy_for_each(shard, axis):
    devices = lax.axis_size(axis)
    return lax.all_to_all(
        jnp.broadcast_to(shard[None], (devices, *shard.shape)), axis, 0, 0, tiled=True
    )


def taken_together(shard, axis):
    return copy_for_each(shard, axis).sum(axis=0)


def laid_out(tiles, dim):
    tiles = jnp.moveaxis(tiles, 0, dim)
    shape = tiles.shape
    return tiles.reshape(*shape[:dim], shape[dim] * shape[dim + 1], *shape[dim + 2 :])


def gathered_copies(shard, axis, dim):
    tiles = copy_for_each(shard, axis)
    return laid_out(tiles, dim)


def smooth(sums, counts, day_dev):
    spilled = passed_along((sums[day_dev:], counts[day_dev:]), "day", 1)
    own_sums = jnp.concatenate([sums[:1] + spilled[0], sums[1:day_dev]], axis=0)
    own_counts = jnp.concatenate([counts[:1] + spilled[1], counts[1:day_dev]], axis=0)
    pieces = {}
    left_keep = HALF - day_dev
    right_keep = HALF - day_dev + 1
    for distance in (1, -1):
        pieces[distance] = passed_along((own_sums, own_counts), "day", distance)
    edge_parts = (
        (2, own_sums[day_dev - left_keep :], own_counts[day_dev - left_keep :]),
        (-2, own_sums[:right_keep], own_counts[:right_keep]),
    )
    for distance, edge_sums, edge_counts in edge_parts:
        pieces[distance] = passed_along((edge_sums, edge_counts), "day", distance)
    before = left_keep + day_dev
    order = (2, 1, 0, -1, -2)
    long_sums = jnp.concatenate(
        [own_sums if distance == 0 else pieces[distance][0] for distance in order], axis=0
    )
    long_counts = jnp.concatenate(
        [own_counts if distance == 0 else pieces[distance][1] for distance in order], axis=0
    )
    total_rows = long_sums.shape[0]
    target_rows = lax.broadcasted_iota(jnp.int32, (day_dev + 1, total_rows), 0) + before
    source_rows = lax.broadcasted_iota(jnp.int32, (day_dev + 1, total_rows), 1)
    band_matrix = (jnp.abs(source_rows - target_rows) <= HALF).astype(jnp.float32)
    hours, share_cells = (sums.shape[1], sums.shape[2])
    window_sums = jnp.dot(
        band_matrix,
        long_sums.reshape(total_rows, hours * share_cells),
        precision=lax.Precision.HIGHEST,
        preferred_element_type=jnp.float32,
    )
    window_counts = jnp.dot(
        band_matrix,
        long_counts,
        precision=lax.Precision.HIGHEST,
        preferred_element_type=jnp.float32,
    )
    return window_sums.reshape(day_dev + 1, hours, share_cells) / window_counts[:, :, None]


def local(field, day_index, sample_count):
    year_dev, day_dev, hours, cells = field.shape
    n_days = day_dev * lax.axis_size("day")
    first_day = lax.axis_index("day") * day_dev
    offsets = jnp.mod(day_index - first_day, n_days)
    columns = lax.broadcasted_iota(jnp.int32, (1, 1, day_dev + 1), 2)
    chosen = (offsets[:, :, None] == columns).astype(jnp.float32)
    selector = chosen[:, :, None, :] * sample_count[:, :, :, None].astype(jnp.float32)
    partial_sums = jnp.einsum(
        "yshe,yshc->ehc", selector.astype(jnp.bfloat16), field, preferred_element_type=jnp.float32
    )
    partial_counts = jnp.transpose(jnp.sum(selector, axis=(0, 1)))
    sums = sent_and_summed(partial_sums, "year", 2)
    counts = taken_together(partial_counts, "year")
    climate_share = smooth(sums, counts, day_dev)
    share = climate_share[:day_dev]
    climate = gathered_copies(climate_share, "year", 2)
    slot_rows = lax.broadcasted_iota(jnp.int32, (year_dev, day_dev), 1)
    unshifted = (offsets == slot_rows)[:, :, None, None]
    selected = jnp.where(unshifted, climate[None, :day_dev], climate[None, 1:])
    anomaly = (field.astype(jnp.float32) - selected).astype(jnp.bfloat16)
    return (anomaly, share.astype(jnp.bfloat16))


def solution(mesh):
    return jax.shard_map(
        local,
        mesh=mesh,
        in_specs=(P("year", "day", None, None), P("year", "day"), P("year", "day", None)),
        out_specs=(P("year", "day", None, None), P("day", None, "year")),
        check_vma=False,
    )
```

profile of v0, /device:TPU:0, one launch (start us, length us, event | category | flops | bytes accessed | tf_op | source)
XLA Modules:
  0.0 146.8 jit_solution(1732856404240386442)
XLA Ops:
  0.6 0.7 convert_element_type.24
  1.3 0.7 iota_compare_fusion.1
  2.0 0.1 multiply_reduce_fusion
  2.1 0.6 broadcast_in_dim.48
  2.7 7.9 %all-to-all-start.1 = ((f32[8,24,2]{1,2,0:T(2,128)}), f32[8,24,2]{1,2,0:T(2,128)S(1)}, u32[]{:S(2)}, u32[]{:S(2)}) async-start(f32[8,24,2]{1,2,0:T(2,128)} %broadcast_in_dim.48), calls=%async_computation.1 | async-start | bytes 16384 | tf_op jit(solution)/shard_map/all_to_all | solution.py:29
  10.6 4.7 %convolution_bitcast_fusion = f32[24,2,11520]{2,0,1:T(8,128)} fusion(bf16[4,23,2,11520]{3,2,1,0:T(2,128)(2,1)} %param.3, f32[4,23,2]{1,0,2:T(4,128)S(1)} %copy.23, f32[4,23,24]{1,2,0:T(8,128)S(1)} %fusion.6), kind=kOutput, calls=%fused_computation | convolution fusion | flops 101753472 | bytes 6460768 | tf_op jit(solution)/shard_map/yshe,yshc->ehc/dot_general | solution.py:100
  15.3 2.9 %reshape.30 = f32[24,2,8,1440]{3,2,0,1:T(8,128)S(1)} reshape(f32[24,2,11520]{2,0,1:T(8,128)} %convolution_bitcast_fusion) | data formatting | bytes 4423680 | tf_op jit(solution)/shard_map/reshape | solution.py:17
  18.3 2.8 %copy.52 = f32[24,2,8,1440]{3,0,1,2:T(8,128)} copy(f32[24,2,8,1440]{3,2,0,1:T(8,128)S(1)} %reshape.30) | data formatting | bytes 4423680 | tf_op jit(solution)/shard_map/reshape | solution.py:17
  21.0 0.0 all-to-all-done.1
  21.0 7.2 %all-to-all-start = ((f32[8,24,2,1440]{3,1,2,0:T(8,128)}), f32[8,24,2,1440]{3,1,2,0:T(8,128)S(1)}, u32[]{:S(2)}, u32[]{:S(2)}) async-start(f32[8,24,2,1440]{3,1,2,0:T(8,128)} %bitcast.24), calls=%async_computation | async-start | bytes 4718592 | tf_op jit(solution)/shard_map/all_to_all | solution.py:23
  28.3 0.1 slice.52
  28.4 0.1 slice.51
  28.4 0.1 slice.49
  28.5 1.6 %collective-permute-start.5 = (f32[7,2]{0,1:T(2,128)S(1)}, f32[7,2]{0,1:T(2,128)S(1)}, u32[]{:S(2)}, u32[]{:S(2)}) collective-permute-start(f32[7,2]{0,1:T(2,128)S(1)} %slice.49), channel_id=1, source_target_pairs={{0,16},{8,24},{16,32},{24,40},{32,48},{40,56},{48,64},{56,72},{64,... | collective-permute-start | bytes 176 | tf_op jit(solution)/shard_map/ppermute | solution.py:12
  30.1 0.0 collective-permute-start.6
  30.1 24.9 %collective-permute-done.6 = f32[1,2]{0,1:T(2,128)S(1)} collective-permute-done((f32[1,2]{0,1:T(2,128)S(1)}, f32[1,2]{0,1:T(2,128)S(1)}, u32[]{:S(2)}, u32[]{:S(2)}) %collective-permute-start.6) | collective-permute-done | bytes 40 | tf_op jit(solution)/shard_map/ppermute | solution.py:12
  55.0 4.0 %all-to-all-done = f32[8,24,2,1440]{3,1,2,0:T(8,128)S(1)} async-done(((f32[8,24,2,1440]{3,1,2,0:T(8,128)}), f32[8,24,2,1440]{3,1,2,0:T(8,128)S(1)}, u32[]{:S(2)}, u32[]{:S(2)}) %all-to-all-start) | async-done | bytes 2211872 | tf_op jit(solution)/shard_map/all_to_all | solution.py:23
  59.0 0.1 reduce_sum.27
  59.2 0.1 collective-permute-start.1
  59.2 0.1 pad_maximum_fusion.1
  59.3 3.8 %collective-permute-start.8 = (f32[23,2]{0,1:T(2,128)S(1)}, f32[23,2]{0,1:T(2,128)S(1)}, u32[]{:S(2)}, u32[]{:S(2)}) collective-permute-start(f32[23,2]{0,1:T(2,128)S(1)} %pad_maximum_fusion.1), channel_id=1, source_target_pairs={{0,120},{8,0},{16,8},{24,16},{32,24},{40,32},{48,40},{56,48},{64,5... | collective-permute-start | bytes 560 | tf_op jit(solution)/shard_map/ppermute | solution.py:12
  63.2 0.0 collective-permute-start.7
  63.2 0.9 collective-permute-start.9
  64.1 0.0 collective-permute-done.5
  64.1 2.6 %collective-permute-done.9 = f32[8,2]{0,1:T(2,128)S(1)} collective-permute-done((f32[8,2]{0,1:T(2,128)S(1)}, f32[8,2]{0,1:T(2,128)S(1)}, u32[]{:S(2)}, u32[]{:S(2)}) %collective-permute-start.9) | collective-permute-done | bytes 96 | tf_op jit(solution)/shard_map/ppermute | solution.py:12
  66.7 0.0 collective-permute-done.8
  66.7 1.5 %collective-permute-done.7 = f32[23,2]{0,1:T(2,128)S(1)} collective-permute-done((f32[23,2]{0,1:T(2,128)S(1)}, f32[23,2]{0,1:T(2,128)S(1)}, u32[]{:S(2)}, u32[]{:S(2)}) %collective-permute-start.7) | collective-permute-done | bytes 216 | tf_op jit(solution)/shard_map/ppermute | solution.py:12
  68.3 0.1 concatenate.17
  68.4 0.1 collective-permute-start
  68.5 0.0 collective-permute-done.1
  68.6 3.4 %collective-permute-start.3 = (f32[23,2,1440]{2,0,1:T(8,128)S(1)}, f32[23,2,1440]{2,0,1:T(8,128)S(1)}, u32[]{:S(2)}, u32[]{:S(2)}) collective-permute-start(f32[23,2,1440]{2,0,1:T(8,128)S(1)} %pad_maximum_fusion), channel_id=1, source_target_pairs={{0,120},{8,0},{16,8},{24,16},{32,24},{40,32},{48,40},{56,48},{64,5... | collective-permute-start | bytes 794888 | tf_op jit(solution)/shard_map/ppermute | solution.py:12
  71.9 0.0 collective-permute-start.2
  71.9 2.0 %collective-permute-start.4 = (f32[8,2,1440]{2,0,1:T(8,128)S(1)}, f32[8,2,1440]{2,0,1:T(8,128)S(1)}, u32[]{:S(2)}, u32[]{:S(2)}) collective-permute-start(f32[8,2,1440]{2,0,1:T(8,128)S(1)} %fusion.3), channel_id=1, source_target_pairs={{0,112},{8,120},{16,0},{24,8},{32,16},{40,24},{48,32},{56,40},{64,... | collective-permute-start | bytes 276488 | tf_op jit(solution)/shard_map/ppermute | solution.py:12
  73.9 0.2 fusion.12
  74.1 1.1 collective-permute-done
  75.2 2.7 %collective-permute-done.4 = f32[8,2,1440]{2,0,1:T(8,128)S(1)} collective-permute-done((f32[8,2,1440]{2,0,1:T(8,128)S(1)}, f32[8,2,1440]{2,0,1:T(8,128)S(1)}, u32[]{:S(2)}, u32[]{:S(2)}) %collective-permute-start.4) | collective-permute-done | bytes 92192 | tf_op jit(solution)/shard_map/ppermute | solution.py:12
  77.9 0.0 collective-permute-done.3
  77.9 2.3 %collective-permute-done.2 = f32[23,2,1440]{2,0,1:T(8,128)S(1)} collective-permute-done((f32[23,2,1440]{2,0,1:T(8,128)S(1)}, f32[23,2,1440]{2,0,1:T(8,128)S(1)}, u32[]{:S(2)}, u32[]{:S(2)}) %collective-permute-start.2) | collective-permute-done | bytes 264992 | tf_op jit(solution)/shard_map/ppermute | solution.py:12
  80.2 1.2 concatenate.15
  81.3 0.8 copy.27
  82.1 1.1 reshape.31
  83.2 1.1 dot_general.15
  84.3 0.6 broadcast_divide_fusion
  84.9 0.2 copy.29
  85.1 2.0 %broadcast_in_dim.49 = f32[8,24,2,1440]{3,2,1,0:T(2,128)} broadcast(f32[24,2,1440]{2,1,0:T(2,128)S(1)} %copy.29), dimensions={1,2,3} | broadcast | bytes 2488320 | tf_op jit(solution)/shard_map/broadcast_in_dim | solution.py:30
  87.1 3.8 %all-to-all-start.2 = ((f32[8,24,2,1440]{3,2,1,0:T(2,128)}), f32[8,24,2,1440]{3,2,1,0:T(2,128)S(1)}, u32[]{:S(2)}, u32[]{:S(2)}) async-start(f32[8,24,2,1440]{3,2,1,0:T(2,128)} %broadcast_in_dim.49), calls=%async_computation.2 | async-start | bytes 4718592 | tf_op jit(solution)/shard_map/all_to_all | solution.py:29
  91.0 0.8 copy.34
  91.8 28.9 %all-to-all-done.2 = f32[8,24,2,1440]{3,2,1,0:T(2,128)S(1)} async-done(((f32[8,24,2,1440]{3,2,1,0:T(2,128)}), f32[8,24,2,1440]{3,2,1,0:T(2,128)S(1)}, u32[]{:S(2)}, u32[]{:S(2)}) %all-to-all-start.2) | async-done | bytes 2211872 | tf_op jit(solution)/shard_map/all_to_all | solution.py:29
  120.6 2.6 %fusion.19 = (f32[23,2,8,1440]{3,1,0,2:T(2,128)S(1)}, f32[23,2,8,1440]{3,1,0,2:T(2,128)}) fusion(f32[24,2,8,1440]{3,1,0,2:T(2,128)S(1)} %bitcast.26), kind=kLoop, calls=%fused_computation.34 | loop fusion | bytes 8478720 | tf_op jit(solution)/shard_map/slice | solution.py:111
  123.2 1.8 %copy.36 = f32[23,2,8,1440]{3,2,1,0:T(8,128)} copy(f32[23,2,8,1440]{3,1,0,2:T(2,128)S(1)} %get-tuple-element.12) | data formatting | bytes 4239360 | tf_op jit(solution)/shard_map/jit(_where)/broadcast_in_dim | solution.py:111
  125.0 0.0 copy-start
  125.0 4.8 %reshape.34 = f32[23,2,11520]{2,1,0:T(2,128)} reshape(f32[23,2,8,1440]{3,2,1,0:T(8,128)} %copy.36) | data formatting | bytes 4239360 | tf_op jit(solution)/shard_map/jit(_where)/broadcast_in_dim | solution.py:111
  129.8 0.0 copy-done
  129.8 1.8 %copy.37 = f32[23,2,8,1440]{3,2,1,0:T(8,128)} copy(f32[23,2,8,1440]{3,1,0,2:T(2,128)S(1)} %copy-done) | data formatting | bytes 4239360 | tf_op jit(solution)/shard_map/jit(_where)/broadcast_in_dim | solution.py:111
  131.5 0.0 copy-start.1
  131.5 4.8 %reshape.35 = f32[23,2,11520]{2,1,0:T(2,128)} reshape(f32[23,2,8,1440]{3,2,1,0:T(8,128)} %copy.37) | data formatting | bytes 4239360 | tf_op jit(solution)/shard_map/jit(_where)/broadcast_in_dim | solution.py:111
  136.4 0.0 copy-done.1
  136.4 10.4 %subtract_convert_fusion = bf16[4,23,2,11520]{3,2,1,0:T(2,128)(2,1)} fusion(bf16[4,23,2,11520]{3,2,1,0:T(2,128)(2,1)} %param.3, pred[4,23]{1,0:T(4,128)(4,1)S(1)} %get-tuple-element.10, f32[23,2,11520]{2,1,0:T(2,128)} %reshape.35, f32[23,2,11520]{2,1,0:T(2,128)S(1)} %copy-done.1), kind=kLoop, calls=%fused_computation.1 | loop fusion | flops 8478720 | bytes 12718172 | tf_op jit(solution)/shard_map/convert_element_type | solution.py:112
  (12 shorter events, 0.2 us)
Async XLA Ops:
  2.7 18.3 %all-to-all-start.1 = ((f32[8,24,2]{1,2,0:T(2,128)}), f32[8,24,2]{1,2,0:T(2,128)S(1)}, u32[]{:S(2)}, u32[]{:S(2)}) async-start(f32[8,24,2]{1,2,0:T(2,128)} %broadcast_in_dim.48), calls=%async_computation.1 | async-start | bytes 16384 | tf_op jit(solution)/shard_map/all_to_all | solution.py:29
  21.0 37.9 %all-to-all-start = ((f32[8,24,2,1440]{3,1,2,0:T(8,128)}), f32[8,24,2,1440]{3,1,2,0:T(8,128)S(1)}, u32[]{:S(2)}, u32[]{:S(2)}) async-start(f32[8,24,2,1440]{3,1,2,0:T(8,128)} %bitcast.24), calls=%async_computation | async-start | bytes 4718592 | tf_op jit(solution)/shard_map/all_to_all | solution.py:23
  28.5 35.6 %collective-permute-start.5 = (f32[7,2]{0,1:T(2,128)S(1)}, f32[7,2]{0,1:T(2,128)S(1)}, u32[]{:S(2)}, u32[]{:S(2)}) collective-permute-start(f32[7,2]{0,1:T(2,128)S(1)} %slice.49), channel_id=1, source_target_pairs={{0,16},{8,24},{16,32},{24,40},{32,48},{40,56},{48,64},{56,72},{64,... | collective-permute-start | bytes 176 | tf_op jit(solution)/shard_map/ppermute | solution.py:12
  30.1 24.9 %collective-permute-start.6 = (f32[1,2]{0,1:T(2,128)S(1)}, f32[1,2]{0,1:T(2,128)S(1)}, u32[]{:S(2)}, u32[]{:S(2)}) collective-permute-start(f32[1,2]{0,1:T(2,128)S(1)} %slice.51), channel_id=1, source_target_pairs={{0,8},{8,16},{16,24},{24,32},{32,40},{40,48},{48,56},{56,64},{64,7... | collective-permute-start | bytes 32 | tf_op jit(solution)/shard_map/ppermute | solution.py:12
  59.2 9.3 %collective-permute-start.1 = (f32[1,2,1440]{2,0,1:T(1,128)S(1)}, f32[1,2,1440]{2,0,1:T(1,128)S(1)}, u32[]{:S(2)}, u32[]{:S(2)}) collective-permute-start(f32[1,2,1440]{2,0,1:T(1,128)S(1)} %slice.59), channel_id=1, source_target_pairs={{0,8},{8,16},{16,24},{24,32},{32,40},{40,48},{48,56},{56,64},{64,7... | collective-permute-start | bytes 34568 | tf_op jit(solution)/shard_map/ppermute | solution.py:12
  59.3 7.4 %collective-permute-start.8 = (f32[23,2]{0,1:T(2,128)S(1)}, f32[23,2]{0,1:T(2,128)S(1)}, u32[]{:S(2)}, u32[]{:S(2)}) collective-permute-start(f32[23,2]{0,1:T(2,128)S(1)} %pad_maximum_fusion.1), channel_id=1, source_target_pairs={{0,120},{8,0},{16,8},{24,16},{32,24},{40,32},{48,40},{56,48},{64,5... | collective-permute-start | bytes 560 | tf_op jit(solution)/shard_map/ppermute | solution.py:12
  63.2 5.1 %collective-permute-start.7 = (f32[23,2]{0,1:T(2,128)S(1)}, f32[23,2]{0,1:T(2,128)S(1)}, u32[]{:S(2)}, u32[]{:S(2)}) collective-permute-start(f32[23,2]{0,1:T(2,128)S(1)} %pad_maximum_fusion.1), channel_id=1, source_target_pairs={{0,8},{8,16},{16,24},{24,32},{32,40},{40,48},{48,56},{56,64},{64,7... | collective-permute-start | bytes 560 | tf_op jit(solution)/shard_map/ppermute | solution.py:12
  63.2 3.6 %collective-permute-start.9 = (f32[8,2]{0,1:T(2,128)S(1)}, f32[8,2]{0,1:T(2,128)S(1)}, u32[]{:S(2)}, u32[]{:S(2)}) collective-permute-start(f32[8,2]{0,1:T(2,128)S(1)} %bitcast.29), channel_id=1, source_target_pairs={{0,112},{8,120},{16,0},{24,8},{32,16},{40,24},{48,32},{56,40},{64,... | collective-permute-start | bytes 200 | tf_op jit(solution)/shard_map/ppermute | solution.py:12
  68.4 6.8 %collective-permute-start = (f32[7,2,1440]{2,0,1:T(8,128)S(1)}, f32[7,2,1440]{2,0,1:T(8,128)S(1)}, u32[]{:S(2)}, u32[]{:S(2)}) collective-permute-start(f32[7,2,1440]{2,0,1:T(8,128)S(1)} %slice.57), channel_id=1, source_target_pairs={{0,16},{8,24},{16,32},{24,40},{32,48},{40,56},{48,64},{56,72},{64,... | collective-permute-start | bytes 241928 | tf_op jit(solution)/shard_map/ppermute | solution.py:12
  68.6 9.3 %collective-permute-start.3 = (f32[23,2,1440]{2,0,1:T(8,128)S(1)}, f32[23,2,1440]{2,0,1:T(8,128)S(1)}, u32[]{:S(2)}, u32[]{:S(2)}) collective-permute-start(f32[23,2,1440]{2,0,1:T(8,128)S(1)} %pad_maximum_fusion), channel_id=1, source_target_pairs={{0,120},{8,0},{16,8},{24,16},{32,24},{40,32},{48,40},{56,48},{64,5... | collective-permute-start | bytes 794888 | tf_op jit(solution)/shard_map/ppermute | solution.py:12
  71.9 8.3 %collective-permute-start.2 = (f32[23,2,1440]{2,0,1:T(8,128)S(1)}, f32[23,2,1440]{2,0,1:T(8,128)S(1)}, u32[]{:S(2)}, u32[]{:S(2)}) collective-permute-start(f32[23,2,1440]{2,0,1:T(8,128)S(1)} %pad_maximum_fusion), channel_id=1, source_target_pairs={{0,8},{8,16},{16,24},{24,32},{32,40},{40,48},{48,56},{56,64},{64,7... | collective-permute-start | bytes 794888 | tf_op jit(solution)/shard_map/ppermute | solution.py:12
  71.9 5.9 %collective-permute-start.4 = (f32[8,2,1440]{2,0,1:T(8,128)S(1)}, f32[8,2,1440]{2,0,1:T(8,128)S(1)}, u32[]{:S(2)}, u32[]{:S(2)}) collective-permute-start(f32[8,2,1440]{2,0,1:T(8,128)S(1)} %fusion.3), channel_id=1, source_target_pairs={{0,112},{8,120},{16,0},{24,8},{32,16},{40,24},{48,32},{56,40},{64,... | collective-permute-start | bytes 276488 | tf_op jit(solution)/shard_map/ppermute | solution.py:12
  87.1 33.5 %all-to-all-start.2 = ((f32[8,24,2,1440]{3,2,1,0:T(2,128)}), f32[8,24,2,1440]{3,2,1,0:T(2,128)S(1)}, u32[]{:S(2)}, u32[]{:S(2)}) async-start(f32[8,24,2,1440]{3,2,1,0:T(2,128)} %broadcast_in_dim.49), calls=%async_computation.2 | async-start | bytes 4718592 | tf_op jit(solution)/shard_map/all_to_all | solution.py:29
  125.0 4.8 %copy-start = (f32[23,2,8,1440]{3,1,0,2:T(2,128)S(1)}, f32[23,2,8,1440]{3,1,0,2:T(2,128)}, u32[]{:S(2)}) copy-start(f32[23,2,8,1440]{3,1,0,2:T(2,128)} %get-tuple-element.13) | copy-start | bytes 6359044
  131.5 4.8 %copy-start.1 = (f32[23,2,11520]{2,1,0:T(2,128)S(1)}, f32[23,2,11520]{2,1,0:T(2,128)}, u32[]{:S(2)}) copy-start(f32[23,2,11520]{2,1,0:T(2,128)} %reshape.34) | copy-start | bytes 6359044
where the time goes:
time: 148 us; the launch traced here: 147 us
  waiting for transfers between devices  68 us (46%)
  starting transfers between devices  30.8 us (21%)
  local copies, waits for them, and re-layouts  29.6 us (20%)
  other arithmetic  12.2 us (8%)
  matrix products  5.45 us (4%)
    ppermute x10, waiting for transfers between devices, passed_along(): return lax.ppermute(value, axis, pairs)  35.2 us
    all_to_all x2, waiting for transfers between devices, copy_for_each(): lax.all_to_all(jnp.broadcast_to(shard[None], (devices, *shard.shape)), ax...  28.9 us
    broadcast_in_dim x4, local copies, waits for them, and re-layouts, local(): selected = jnp.where(unshifted, climate[None, :day_dev], climate[None, 1:])  13.2 us
    ppermute x10, starting transfers between devices, passed_along(): return lax.ppermute(value, axis, pairs)  11.8 us
    all_to_all x2, starting transfers between devices, copy_for_each(): lax.all_to_all(jnp.broadcast_to(shard[None], (devices, *shard.shape)), ax...  11.7 us
    convert_element_type x1, other arithmetic, local(): anomaly = (field.astype(jnp.float32) - selected).astype(jnp.bfloat16)  10.4 us
    all_to_all x1, starting transfers between devices, sent_and_summed(): lax.all_to_all(in_blocks(shard, dim, devices), axis, 0, 0, tiled=True)  7.21 us
    reshape x2, local copies, waits for them, and re-layouts, in_blocks(): shard.reshape(*shape[:dim], devices, shape[dim] // devices, *shape[dim +...  5.7 us
  transfers between devices with their start and end apart: 13, of which 8 were waited for; matrix products, arithmetic and copies ran while one was open for 8% of the time, Pallas kernels for 0%

commit v1 on v0

v1 whole, which is shorter than its diff:
```python
import functools

import jax
import jax.numpy as jnp
from jax import lax
from jax.experimental import pallas as pl
from jax.experimental.layout import Layout, with_layout_constraint
from jax.experimental.pallas import tpu as pltpu
from jax.sharding import PartitionSpec as P

MESH = pl.DeviceIdType.MESH
HALF = 30
YEARS, DAYS, HOURS, TILES = 4, 23, 2, 90
LANES = 128
ROWS = DAYS + 1
MID = ROWS // 2
SLOT, FIRST, SECOND = 23, 13, 10
SHARE, SKIP = 7, 6
MESSAGES = 64


def lanes(start, tiles):
    return pl.ds(pl.multiple_of(start * LANES, LANES), tiles * LANES)


def rows_of(low):
    return pl.ds(0, MID) if low else pl.ds(MID, MID)


def reduce_kernel(
    field, count_ref, index_ref, cl, held, part, weight, first_count, second_count,
    count0, count1, count2, count_x, count_z, count_d, first_in, second_in, second_x, first_x,
    first_share, second_share, first_win, second_win, kept, inverse, load_sem, send_sem, recv_sem,
):
    day = lax.axis_index("day")
    year = lax.axis_index("year")
    days = lax.axis_size("day")
    z, u = year // 2, year % 2
    up, down, across = (z + 1) % 4, (z + 3) % 4, (z + 2) % 4
    at_up, at_down, at_across = (day, up * 2 + u), (day, down * 2 + u), (day, across * 2 + u)
    twin = (day, z * 2 + (1 - u))
    beside = [((day + step + days) % days, year) for step in (1, -1, 2, -2)]
    peers = [at_up, at_down, at_across, twin] + beside

    barrier = pltpu.get_barrier_semaphore()
    for peer in peers:
        pl.semaphore_signal(barrier, inc=1, device_id=peer, device_id_type=MESH)

    pieces = [(0, 24), (24, 24), (48, 24), (72, 18)]
    loads = []
    for number, (start, tiles) in enumerate(pieces):
        span = pl.ds(start * LANES, tiles * LANES)
        load = pltpu.make_async_copy(
            field.at[:, :, :, span], held.at[:, :, :, span], load_sem.at[number]
        )
        load.start()
        loads.append(load)

    used = []

    def copy(source, target, device):
        number = len(used)
        used.append(
            pltpu.make_async_remote_copy(
                src_ref=source, dst_ref=target, send_sem=send_sem.at[number],
                recv_sem=recv_sem.at[number], device_id=device, device_id_type=MESH,
            )
        )
        used[-1].start()
        return used[-1]

    slot = lax.broadcasted_iota(jnp.int32, (YEARS, DAYS), 1) + day * DAYS
    moved = (index_ref[...] != slot).astype(jnp.float32)
    total_own = jnp.zeros((HOURS, DAYS), jnp.float32)
    total_next = jnp.zeros((HOURS, DAYS), jnp.float32)
    for y in range(YEARS):
        counts = count_ref[y].astype(jnp.float32)
        after = counts * moved[y : y + 1, :]
        own = counts - after
        total_own += own
        total_next += after
        for s in range(DAYS):
            weight[y, s] = jnp.broadcast_to(own[:, s : s + 1], (HOURS, 4 * LANES))
            weight[y, DAYS + s] = jnp.broadcast_to(after[:, s : s + 1], (HOURS, 4 * LANES))
    first_count[...] = jnp.zeros_like(first_count)
    second_count[...] = jnp.zeros_like(second_count)
    first_count[:, :DAYS] = total_own
    second_count[:, :DAYS] = total_next
    count0[...] = first_count[...] + pltpu.roll(second_count[...], 1, 1)

    def add_years(start, tiles):
        halves = [(h, min(4, tiles - h)) for h in range(0, tiles, 4)]
        carried = [None] * len(halves)
        for s in range(DAYS):
            own = [None] * len(halves)
            after = [None] * len(halves)
            for y in range(YEARS):
                value = held[y, s, :, lanes(start, tiles)].astype(jnp.float32)
                for n, (h, width) in enumerate(halves):
                    piece = value[:, h * LANES : (h + width) * LANES]
                    a = piece * weight[y, s, :, : width * LANES]
                    b = piece * weight[y, DAYS + s, :, : width * LANES]
                    own[n] = a if y == 0 else own[n] + a
                    after[n] = b if y == 0 else after[n] + b
            for n, (h, width) in enumerate(halves):
                row = own[n] if s == 0 else own[n] + carried[n]
                part[s, :, lanes(start + h, width)] = row
            carried = after
        for n, (h, width) in enumerate(halves):
            part[DAYS, :, lanes(start + h, width)] = carried[n]

    part[:, :, TILES * LANES :] = jnp.zeros((ROWS, HOURS, (4 * SLOT - TILES) * LANES), jnp.float32)
    for (start, tiles), load in zip(pieces, loads):
        load.wait()

        @pl.loop(0, tiles // 8)
        def _(step):
            add_years(start + step * 8, 8)

        if tiles % 8:
            add_years(start + tiles // 8 * 8, tiles % 8)

    pl.semaphore_wait(barrier, len(peers))

    def first_at(s):
        return s * SLOT

    def second_at(s):
        return s * SLOT + FIRST

    class Ring:
        def __init__(self, buffers, at, tiles):
            self.buffers, self.at, self.tiles = buffers, at, tiles

        def piece(self, low, s):
            return part.at[rows_of(low), :, lanes(self.at(s), self.tiles)]

        def begin(self):
            self.far_up = copy(self.piece(True, across), self.buffers.at[0], at_up)
            self.far_down = copy(self.piece(False, across), self.buffers.at[1], at_down)

        def near_up(self):
            self.up = copy(self.piece(False, up), self.buffers.at[2], at_up)

        def near_down(self):
            self.down = copy(self.piece(True, down), self.buffers.at[3], at_down)

        def forward(self):
            self.far_up.wait_recv()
            self.add(True, up, 0)
            self.on_up = copy(self.piece(True, up), self.buffers.at[4], at_up)
            self.far_down.wait_recv()
            self.add(False, down, 1)
            self.on_down = copy(self.piece(False, down), self.buffers.at[5], at_down)

        def add(self, low, s, number):
            where = (rows_of(low), slice(None), lanes(self.at(s), self.tiles))
            part[where] = part[where] + self.buffers[number]

        def result(self):
            self.up.wait_recv()
            self.down.wait_recv()
            self.on_up.wait_recv()
            self.on_down.wait_recv()
            where = lanes(self.at(z), self.tiles)
            low = part[rows_of(True), :, where] + self.buffers[3] + self.buffers[4]
            high = part[rows_of(False), :, where] + self.buffers[2] + self.buffers[5]
            return low, high

    first = Ring(first_in, first_at, FIRST)
    second = Ring(second_in, lambda s: second_at(s) + u * (SECOND // 2), SECOND // 2)

    send_count = copy(count0, count_x, twin)
    first.begin()
    swaps = []
    order = (across, up, down, z)
    for number, s in enumerate(order):
        source = part.at[:, :, lanes(second_at(s) + (1 - u) * (SECOND // 2), SECOND // 2)]
        swaps.append(copy(source, second_x.at[number], twin))
    first.near_up()
    first.near_down()

    def swapped(number):
        swaps[number].wait_recv()
        where = (slice(None), slice(None), lanes(second.at(order[number]), SECOND // 2))
        part[where] = part[where] + second_x[number]

    send_count.wait_recv()
    count1[...] = count0[...] + count_x[...]
    along = [copy(count1, count_z.at[n], d) for n, d in enumerate((at_up, at_down, at_across))]

    first.forward()
    swapped(0)
    second.begin()
    swapped(1)
    second.near_up()
    swapped(2)
    second.near_down()
    for message in along:
        message.wait_recv()
    count2[...] = count1[...] + count_z[0] + count_z[1] + count_z[2]
    aside = [copy(count2, count_d.at[n], d) for n, d in enumerate(beside)]
    second.forward()

    low, high = first.result()
    part[rows_of(True), :, lanes(first_at(z), FIRST)] = low
    part[rows_of(False), :, lanes(first_at(z), FIRST)] = high
    swap_first = copy(part.at[:, :, lanes(first_at(z) + (1 - u) * SKIP, SHARE)], first_x, twin)

    swapped(3)
    low, high = second.result()
    second_share[rows_of(True)] = low
    second_share[rows_of(False)] = high

    def share_out(share, window):
        right, left, right2, left2 = beside
        edge = ROWS // 3
        return [
            copy(share, window.at[pl.ds(0, ROWS)], right),
            copy(share, window.at[pl.ds(ROWS, ROWS)], left),
            copy(share.at[pl.ds(ROWS - edge, edge)], window.at[pl.ds(2 * ROWS, edge)], right2),
            copy(share.at[pl.ds(0, edge)], window.at[pl.ds(2 * ROWS + edge, edge)], left2),
        ]

    second_out = share_out(second_share, second_win)
    swap_first.wait_recv()
    first_share[...] = part[:, :, lanes(first_at(z) + u * SKIP, SHARE)] + first_x[...]
    first_out = share_out(first_share, first_win)

    for message in aside:
        message.wait_recv()
    spread = (
        count_d[2]
        + pltpu.roll(count_d[0], DAYS, 1)
        + pltpu.roll(count2[...], 2 * DAYS, 1)
        + pltpu.roll(count_d[1], 3 * DAYS, 1)
        + pltpu.roll(count_d[3], 4 * DAYS, 1)
    )
    lane = lax.broadcasted_iota(jnp.int32, (HOURS, LANES), 1)
    for i in range(ROWS):
        start = 2 * DAYS - HALF + i
        inside = (lane >= start) & (lane <= start + 2 * HALF)
        count = jnp.sum(jnp.where(inside, spread, 0.0), axis=1, keepdims=True)
        inverse[i] = jnp.broadcast_to(1.0 / count, (HOURS, 4 * LANES))

    def smooth(messages, share, window, at, tiles):
        for message in messages:
            message.wait_recv()
        edge = ROWS // 3

        def day_row(offset, span):
            def own(r):
                return share[r, :, span]

            def back(r):
                return window[r, :, span]

            def ahead(r):
                return window[ROWS + r, :, span]

            if offset < -DAYS:
                return window[2 * ROWS + offset + 2 * DAYS - (ROWS - edge), :, span]
            if offset == -DAYS:
                return back(0) + window[2 * ROWS + edge - 1, :, span]
            if offset < 0:
                return back(offset + DAYS)
            if offset == 0:
                return own(0) + back(DAYS)
            if offset < DAYS:
                return own(offset)
            if offset == DAYS:
                return ahead(0) + own(DAYS)
            if offset < 2 * DAYS:
                return ahead(offset - DAYS)
            if offset == 2 * DAYS:
                return window[2 * ROWS + edge, :, span] + ahead(DAYS)
            return window[2 * ROWS + edge + offset - 2 * DAYS, :, span]

        for h in range(0, tiles, 4):
            width = min(4, tiles - h)
            span = pl.ds(h * LANES, width * LANES)
            total = day_row(0, span)
            for offset in range(1, DAYS):
                total = total + day_row(offset, span)
            for offset in range(-1, -HALF - 1, -1):
                total = total + day_row(offset, span)
                if offset + HALF < ROWS:
                    kept[offset + HALF, :, : width * LANES] = total
            total = None
            for offset in range(DAYS, DAYS + HALF + 1):
                row = day_row(offset, span)
                total = row if total is None else total + row
                if offset >= HALF:
                    i = offset - HALF
                    sums = kept[i, :, : width * LANES] + total
                    cl[i, :, lanes(at + h, width)] = sums * inverse[i, :, : width * LANES]

    class Spread:
        def __init__(self, at, tiles):
            self.at, self.tiles = at, tiles

        def send(self, low, s, device):
            piece = cl.at[rows_of(low), :, lanes(self.at(s), self.tiles)]
            return copy(piece, piece, device)

        def begin(self):
            self.up0 = self.send(True, z, at_up)
            self.down0 = self.send(False, z, at_down)
            self.up1 = self.send(False, z, at_up)
            self.down1 = self.send(True, z, at_down)

        def forward(self):
            self.up0.wait_recv()
            self.up2 = self.send(True, down, at_up)
            self.down0.wait_recv()
            self.down2 = self.send(False, up, at_down)

        def near(self):
            self.up1.wait_recv()
            self.down1.wait_recv()

        def far(self):
            self.up2.wait_recv()
            self.down2.wait_recv()

    def across_x(s):
        piece = cl.at[:, :, lanes(second_at(s) + u * (SECOND // 2), SECOND // 2)]
        return copy(piece, piece, twin)

    second_spread = Spread(lambda s: second_at(s) + u * (SECOND // 2), SECOND // 2)
    own_spread = Spread(lambda s: first_at(s) + u * SKIP, SHARE)
    other_spread = Spread(lambda s: first_at(s) + (1 - u) * SHARE, SKIP)

    smooth(second_out, second_share, second_win, second_at(z) + u * (SECOND // 2), SECOND // 2)
    second_spread.begin()
    last = [across_x(z)]
    smooth(first_out, first_share, first_win, first_at(z) + u * SKIP, SHARE)
    piece = cl.at[:, :, lanes(first_at(z) + u * SHARE, SKIP)]
    to_twin = copy(piece, piece, twin)
    own_spread.begin()
    second_spread.forward()
    second_spread.near()
    last += [across_x(up), across_x(down)]
    to_twin.wait_recv()
    other_spread.begin()
    own_spread.forward()
    second_spread.far()
    last += [across_x(across)]
    other_spread.forward()
    for spread_portion in (own_spread, other_spread):
        spread_portion.near()
        spread_portion.far()
    for message in last:
        message.wait_recv()
    for message in used:
        message.wait_send()


def climate_of(field, day_index, counts):
    f32 = jnp.float32
    wide = 4 * SLOT * LANES
    vmem = pltpu.VMEM
    row = (HOURS, LANES)
    edge = ROWS // 3
    scratch = [
        vmem((YEARS, DAYS, HOURS, TILES * LANES), jnp.bfloat16),
        vmem((ROWS, HOURS, wide), f32),
        vmem((YEARS, 2 * DAYS, HOURS, 4 * LANES), f32),
        vmem(row, f32), vmem(row, f32), vmem(row, f32), vmem(row, f32), vmem(row, f32),
        vmem(row, f32), vmem((3, *row), f32), vmem((4, *row), f32),
        vmem((6, MID, HOURS, FIRST * LANES), f32),
        vmem((6, MID, HOURS, SECOND // 2 * LANES), f32),
        vmem((4, ROWS, HOURS, SECOND // 2 * LANES), f32),
        vmem((ROWS, HOURS, SHARE * LANES), f32),
        vmem((ROWS, HOURS, SHARE * LANES), f32),
        vmem((ROWS, HOURS, SECOND // 2 * LANES), f32),
        vmem((2 * ROWS + 2 * edge, HOURS, SHARE * LANES), f32),
        vmem((2 * ROWS + 2 * edge, HOURS, SECOND // 2 * LANES), f32),
        vmem((ROWS, HOURS, 4 * LANES), f32),
        vmem((ROWS, HOURS, 4 * LANES), f32),
        pltpu.SemaphoreType.DMA((4,)),
        pltpu.SemaphoreType.DMA((MESSAGES,)),
        pltpu.SemaphoreType.DMA((MESSAGES,)),
    ]
    return pl.pallas_call(
        reduce_kernel,
        out_shape=jax.ShapeDtypeStruct((ROWS, HOURS, wide), f32),
        in_specs=[
            pl.BlockSpec(memory_space=pl.ANY),
            pl.BlockSpec(memory_space=vmem),
            pl.BlockSpec(memory_space=vmem),
        ],
        out_specs=pl.BlockSpec(memory_space=vmem),
        scratch_shapes=scratch,
        compiler_params=pltpu.CompilerParams(
            collective_id=0, has_side_effects=True, vmem_limit_bytes=40 * 2**20
        ),
        name="climate",
    )(field, counts, day_index)


STRIP = HOURS * TILES
WIDE = HOURS * 4 * SLOT
PAIRS = YEARS * DAYS // 2
GROUP = 2


def subtract_kernel(index_ref, field, climate, out, moved_on, held, ready, load_sem, store_sem):
    day = lax.axis_index("day")
    size = GROUP * 2 * STRIP
    groups = PAIRS // GROUP
    loads = [
        pltpu.make_async_copy(
            field.at[pl.ds(g * size, size)], held.at[pl.ds(g * size, size)], load_sem.at[g]
        )
        for g in range(groups)
    ]
    for load in loads:
        load.start()

    @pl.loop(0, ROWS)
    def _(e):
        base = pl.multiple_of(e * (WIDE + 8), 8)
        value = climate[pl.ds(pl.multiple_of(e * WIDE, 8), STRIP), :]
        moved_on[pl.ds(base + 4, STRIP), :] = value

    sublane = lax.broadcasted_iota(jnp.int32, (8, LANES), 0)

    def row_of(k):
        y, s = divmod(k, DAYS)
        ahead = (index_ref[y, s] != day * DAYS + s).astype(jnp.int32)
        return s + ahead

    stores = []
    body = STRIP - STRIP % 8
    for g in range(groups):
        loads[g].wait()
        for pair in range(g * GROUP, (g + 1) * GROUP):
            start = pair * 2 * STRIP
            even = pl.multiple_of(row_of(2 * pair) * WIDE, 8)
            odd = pl.multiple_of(row_of(2 * pair + 1) * (WIDE + 8), 8)

            def put(offset, size, value):
                span = pl.ds(start + offset, size)
                ready[span, :] = (held[span, :].astype(jnp.float32) - value).astype(jnp.bfloat16)

            put(0, body, climate[pl.ds(even, body), :])
            middle = jnp.where(
                sublane < 4, climate[pl.ds(even + body, 8), :], moved_on[pl.ds(odd, 8), :]
            )
            put(body, 8, middle)
            put(body + 8, body, moved_on[pl.ds(odd + 8, body), :])
        store = pltpu.make_async_copy(
            ready.at[pl.ds(g * size, size)], out.at[pl.ds(g * size, size)], store_sem.at[g]
        )
        store.start()
        stores.append(store)
    for store in stores:
        store.wait()


def anomaly_of(field, day_index, climate):
    rows = YEARS * DAYS * STRIP
    groups = PAIRS // GROUP
    return pl.pallas_call(
        subtract_kernel,
        out_shape=jax.ShapeDtypeStruct((rows, LANES), jnp.bfloat16),
        in_specs=[
            pl.BlockSpec(memory_space=pltpu.SMEM),
            pl.BlockSpec(memory_space=pl.ANY),
            pl.BlockSpec(memory_space=pltpu.VMEM),
        ],
        out_specs=pl.BlockSpec(memory_space=pl.ANY),
        scratch_shapes=[
            pltpu.VMEM((ROWS * (WIDE + 8), LANES), jnp.float32),
            pltpu.VMEM((rows, LANES), jnp.bfloat16),
            pltpu.VMEM((rows, LANES), jnp.bfloat16),
            pltpu.SemaphoreType.DMA((groups,)),
            pltpu.SemaphoreType.DMA((groups,)),
        ],
        compiler_params=pltpu.CompilerParams(vmem_limit_bytes=40 * 2**20),
        name="anomaly",
    )(day_index, field, climate)


def tile_rows(array):
    *lead, hours, cells = array.shape
    tiles = cells // LANES
    split = array.reshape(-1, hours, tiles, LANES)
    split = with_layout_constraint(split, Layout(major_to_minor=(0, 2, 1, 3)))
    return split.transpose(0, 2, 1, 3).reshape(-1, LANES)


def from_tile_rows(rows, shape):
    *lead, hours, cells = shape
    tiles = cells // LANES
    split = rows.reshape(-1, tiles, hours, LANES).transpose(0, 2, 1, 3)
    split = with_layout_constraint(split, Layout(major_to_minor=(0, 2, 1, 3)))
    return split.reshape(shape)


def local(field, day_index, sample_count):
    climate = climate_of(field, day_index, jnp.transpose(sample_count, (0, 2, 1)))
    anomaly = anomaly_of(tile_rows(field), day_index, tile_rows(climate))
    anomaly = from_tile_rows(anomaly, field.shape)
    cells = TILES * LANES // lax.axis_size("year")
    share = lax.dynamic_slice(
        climate, (0, 0, lax.axis_index("year") * cells), (DAYS, HOURS, cells)
    )
    return anomaly, share.astype(jnp.bfloat16)


def solution(mesh):
    return jax.shard_map(
        local,
        mesh=mesh,
        in_specs=(P("year", "day", None, None), P("year", "day"), P("year", "day", None)),
        out_specs=(P("year", "day", None, None), P("day", None, "year")),
        check_vma=False,
    )
```

time: 148 us -> 63 us (0.43)
  waiting for transfers between devices: 68 us -> 0 us
  Pallas kernels: 0 us -> 57.3 us
  starting transfers between devices: 30.8 us -> 0 us
  local copies, waits for them, and re-layouts: 29.6 us -> 4.45 us
  other arithmetic: 12.2 us -> 0 us
  matrix products: 5.45 us -> 0 us
    pallas_call x0 -> x2, Pallas kernels: none -> 57.3 us  [the longest x1 48.6 us: climate_of(): pl.pallas_call(reduce_kernel, out_shape=jax.ShapeDtypeStruct((ROWS, HOURS...]
    ppermute x10 -> x0, waiting for transfers between devices: 35.2 us -> none  [passed_along(): return lax.ppermute(value, axis, pairs)]
    all_to_all x3 -> x0, waiting for transfers between devices: 32.9 us -> none  [the longest x2 28.9 us: copy_for_each(): lax.all_to_all(jnp.broadcast_to(shard[None], (devices, *shard.shape)), ax...]
    all_to_all x3 -> x0, starting transfers between devices: 18.9 us -> none  [the longest x2 11.7 us: copy_for_each(): lax.all_to_all(jnp.broadcast_to(shard[None], (devices, *shard.shape)), ax...]
    broadcast_in_dim x6 -> x0, local copies, waits for them, and re-layouts: 15.8 us -> none  [the longest x4 13.2 us: local(): selected = jnp.where(unshifted, climate[None, :day_dev], climate[None, 1:])]
    ppermute x10 -> x0, starting transfers between devices: 11.8 us -> none  [passed_along(): return lax.ppermute(value, axis, pairs)]
    convert_element_type x3 -> x0, other arithmetic: 11.1 us -> none  [the longest x1 10.4 us: local(): anomaly = (field.astype(jnp.float32) - selected).astype(jnp.bfloat16)]
    reshape x3 -> x0, local copies, waits for them, and re-layouts: 6.77 us -> none  [the longest x2 5.7 us: in_blocks(): shard.reshape(*shape[:dim], devices, shape[dim] // devices, *shape[dim +...]
  transfers between devices with their start and end apart: 13 -> 0, of which waited for: 8 -> 0; matrix products, arithmetic and copies ran while one was open for 8% -> 0% of each run, Pallas kernels for 0% -> 0%
where the time goes in v1:
time: 63 us; the launch traced here: 62.4 us
  Pallas kernels  57.3 us (91%)
  local copies, waits for them, and re-layouts  4.45 us (7%)
  between operations  0.65 us (1%)
    pallas_call x1, Pallas kernels, climate_of(): pl.pallas_call(reduce_kernel, out_shape=jax.ShapeDtypeStruct((ROWS, HOURS...  48.6 us
    pallas_call x1, Pallas kernels, anomaly_of(): pl.pallas_call(subtract_kernel, out_shape=jax.ShapeDtypeStruct((rows, LAN...  8.69 us
    unnamed x6, local copies, waits for them, and re-layouts  3.56 us

profile of v1, /device:TPU:0, one launch (start us, length us, event | category | flops | bytes accessed | tf_op | source)
XLA Modules:
  0.0 62.4 jit_solution(8848537310009730010)
XLA Ops:
  0.6 0.0 copy-start
  0.6 2.2 %copy-done = bf16[4,23,2,11520]{3,2,1,0:T(2,128)(2,1)S(1)} copy-done((bf16[4,23,2,11520]{3,2,1,0:T(2,128)(2,1)S(1)}, bf16[4,23,2,11520]{3,2,1,0:T(2,128)(2,1)}, u32[]{:S(2)}) %copy-start) | copy-done | bytes 4239384
  2.8 0.0 copy-start.1
  2.8 0.7 %copy-done.1 = s32[4,23]{1,0:T(4,128)S(1)} copy-done((s32[4,23]{1,0:T(4,128)S(1)}, s32[4,23]{1,0:T(4,128)}, u32[]{:S(2)}) %copy-start.1) | copy-done | bytes 392
  3.5 0.0 copy-start.2
  3.5 0.7 %copy-done.2 = s32[4,23,2]{1,2,0:T(2,128)S(1)} copy-done((s32[4,23,2]{1,2,0:T(2,128)S(1)}, s32[4,23,2]{1,2,0:T(2,128)}, u32[]{:S(2)}) %copy-start.2) | copy-done | bytes 760
  4.2 48.6 %climate.1 = f32[24,2,11776]{2,1,0:T(2,128)S(1)} custom-call(bf16[4,23,2,11520]{3,2,1,0:T(2,128)(2,1)S(1)} %copy-done, s32[4,2,23]{2,1,0:T(2,128)S(1)} %bitcast.18, s32[4,23]{1,0:T(4,128)S(1)} %copy-done.1), custom_call_target="tpu_custom_call" | custom-call | tf_op jit(solution)/shard_map/climate/pallas_call | solution.py:385
  52.8 0.9 %dynamic-slice_convert_fusion = bf16[23,2,1440]{2,1,0:T(2,128)(2,1)} fusion(f32[24,2,11776]{2,1,0:T(2,128)S(1)} %climate.1, s32[]{:T(128)S(6)} %select_n.3), kind=kLoop, calls=%fused_computation | loop fusion | bytes 264964 | tf_op jit(solution)/shard_map/convert_element_type | solution.py:510
  53.7 8.7 %anomaly.1 = bf16[16560,128]{1,0:T(8,128)(2,1)} custom-call(s32[4,23]{1,0:T(4,128)S(1)} %copy-done.1, bf16[16560,128]{1,0:T(8,128)(2,1)S(1)} %bitcast.16, f32[4416,128]{1,0:T(8,128)S(1)} %bitcast.17), custom_call_target="tpu_custom_call" | custom-call | tf_op jit(solution)/shard_map/anomaly/pallas_call | solution.py:465
Async XLA Ops:
  0.6 2.2 %copy-start = (bf16[4,23,2,11520]{3,2,1,0:T(2,128)(2,1)S(1)}, bf16[4,23,2,11520]{3,2,1,0:T(2,128)(2,1)}, u32[]{:S(2)}) copy-start(bf16[4,23,2,11520]{3,2,1,0:T(2,128)(2,1)} %field.1) | copy-start | bytes 12718084
  2.8 0.7 %copy-start.1 = (s32[4,23]{1,0:T(4,128)S(1)}, s32[4,23]{1,0:T(4,128)}, u32[]{:S(2)}) copy-start(s32[4,23]{1,0:T(4,128)} %index_ref.3) | copy-start | bytes 1108
  3.5 0.7 %copy-start.2 = (s32[4,23,2]{1,2,0:T(2,128)S(1)}, s32[4,23,2]{1,2,0:T(2,128)}, u32[]{:S(2)}) copy-start(s32[4,23,2]{1,2,0:T(2,128)} %param.5) | copy-start | bytes 2212

commit v2 on v1

--- a/solution.py
+++ b/solution.py
@@ -28,7 +28,7 @@
 
 
 def reduce_kernel(
-    field, count_ref, index_ref, cl, held, part, weight, first_count, second_count,
+    field, count_ref, cl, held, part, weight, first_count, second_count,
     count0, count1, count2, count_x, count_z, count_d, first_in, second_in, second_x, first_x,
     first_share, second_share, first_win, second_win, kept, inverse, load_sem, send_sem, recv_sem,
 ):
@@ -69,14 +69,12 @@
         used[-1].start()
         return used[-1]
 
-    slot = lax.broadcasted_iota(jnp.int32, (YEARS, DAYS), 1) + day * DAYS
-    moved = (index_ref[...] != slot).astype(jnp.float32)
     total_own = jnp.zeros((HOURS, DAYS), jnp.float32)
     total_next = jnp.zeros((HOURS, DAYS), jnp.float32)
     for y in range(YEARS):
         counts = count_ref[y].astype(jnp.float32)
-        after = counts * moved[y : y + 1, :]
-        own = counts - after
+        own = jnp.maximum(counts, 0.0)
+        after = jnp.maximum(-counts, 0.0)
         total_own += own
         total_next += after
         for s in range(DAYS):
@@ -356,14 +354,13 @@
         message.wait_send()
 
 
-def climate_of(field, day_index, counts):
+def climate_of(field, counts):
     f32 = jnp.float32
     wide = 4 * SLOT * LANES
     vmem = pltpu.VMEM
     row = (HOURS, LANES)
     edge = ROWS // 3
     scratch = [
-        vmem((YEARS, DAYS, HOURS, TILES * LANES), jnp.bfloat16),
         vmem((ROWS, HOURS, wide), f32),
         vmem((YEARS, 2 * DAYS, HOURS, 4 * LANES), f32),
         vmem(row, f32), vmem(row, f32), vmem(row, f32), vmem(row, f32), vmem(row, f32),
@@ -384,19 +381,21 @@
     ]
     return pl.pallas_call(
         reduce_kernel,
-        out_shape=jax.ShapeDtypeStruct((ROWS, HOURS, wide), f32),
+        out_shape=(
+            jax.ShapeDtypeStruct((ROWS, HOURS, wide), f32),
+            jax.ShapeDtypeStruct(field.shape, field.dtype),
+        ),
         in_specs=[
-            pl.BlockSpec(memory_space=pl.ANY),
-            pl.BlockSpec(memory_space=vmem),
+            pl.BlockSpec(memory_space=pltpu.HBM),
             pl.BlockSpec(memory_space=vmem),
         ],
-        out_specs=pl.BlockSpec(memory_space=vmem),
+        out_specs=[pl.BlockSpec(memory_space=vmem)] * 2,
         scratch_shapes=scratch,
         compiler_params=pltpu.CompilerParams(
-            collective_id=0, has_side_effects=True, vmem_limit_bytes=40 * 2**20
+            collective_id=0, has_side_effects=True, vmem_limit_bytes=46 * 2**20
         ),
         name="climate",
-    )(field, counts, day_index)
+    )(field, counts)
 
 
 STRIP = HOURS * TILES
@@ -405,18 +404,9 @@
 GROUP = 2
 
 
-def subtract_kernel(index_ref, field, climate, out, moved_on, held, ready, load_sem, store_sem):
-    day = lax.axis_index("day")
+def subtract_kernel(count_ref, field, climate, out, moved_on, ready, store_sem):
     size = GROUP * 2 * STRIP
     groups = PAIRS // GROUP
-    loads = [
-        pltpu.make_async_copy(
-            field.at[pl.ds(g * size, size)], held.at[pl.ds(g * size, size)], load_sem.at[g]
-        )
-        for g in range(groups)
-    ]
-    for load in loads:
-        load.start()
 
     @pl.loop(0, ROWS)
     def _(e):
@@ -428,13 +418,12 @@
 
     def row_of(k):
         y, s = divmod(k, DAYS)
-        ahead = (index_ref[y, s] != day * DAYS + s).astype(jnp.int32)
+        ahead = (count_ref[y, 0, s] < 0).astype(jnp.int32)
         return s + ahead
 
     stores = []
     body = STRIP - STRIP % 8
     for g in range(groups):
-        loads[g].wait()
         for pair in range(g * GROUP, (g + 1) * GROUP):
             start = pair * 2 * STRIP
             even = pl.multiple_of(row_of(2 * pair) * WIDE, 8)
@@ -442,7 +431,7 @@
 
             def put(offset, size, value):
                 span = pl.ds(start + offset, size)
-                ready[span, :] = (held[span, :].astype(jnp.float32) - value).astype(jnp.bfloat16)
+                ready[span, :] = (field[span, :].astype(jnp.float32) - value).astype(jnp.bfloat16)
 
             put(0, body, climate[pl.ds(even, body), :])
             middle = jnp.where(
@@ -459,7 +448,7 @@
         store.wait()
 
 
-def anomaly_of(field, day_index, climate):
+def anomaly_of(field, counts, climate):
     rows = YEARS * DAYS * STRIP
     groups = PAIRS // GROUP
     return pl.pallas_call(
@@ -467,20 +456,18 @@
         out_shape=jax.ShapeDtypeStruct((rows, LANES), jnp.bfloat16),
         in_specs=[
             pl.BlockSpec(memory_space=pltpu.SMEM),
-            pl.BlockSpec(memory_space=pl.ANY),
+            pl.BlockSpec(memory_space=pltpu.VMEM),
             pl.BlockSpec(memory_space=pltpu.VMEM),
         ],
-        out_specs=pl.BlockSpec(memory_space=pl.ANY),
+        out_specs=pl.BlockSpec(memory_space=pltpu.HBM),
         scratch_shapes=[
             pltpu.VMEM((ROWS * (WIDE + 8), LANES), jnp.float32),
             pltpu.VMEM((rows, LANES), jnp.bfloat16),
-            pltpu.VMEM((rows, LANES), jnp.bfloat16),
-            pltpu.SemaphoreType.DMA((groups,)),
             pltpu.SemaphoreType.DMA((groups,)),
         ],
         compiler_params=pltpu.CompilerParams(vmem_limit_bytes=40 * 2**20),
         name="anomaly",
-    )(day_index, field, climate)
+    )(counts, field, climate)
 
 
 def tile_rows(array):
@@ -500,8 +487,12 @@
 
 
 def local(field, day_index, sample_count):
-    climate = climate_of(field, day_index, jnp.transpose(sample_count, (0, 2, 1)))
-    anomaly = anomaly_of(tile_rows(field), day_index, tile_rows(climate))
+    slot = lax.broadcasted_iota(jnp.int32, day_index.shape, 1) + lax.axis_index("day") * DAYS
+    moved = (day_index != slot)[:, None, :]
+    counts = jnp.transpose(sample_count, (0, 2, 1))
+    counts = jnp.where(moved, -counts, counts)
+    climate, field = climate_of(field, counts)
+    anomaly = anomaly_of(tile_rows(field), counts, tile_rows(climate))
     anomaly = from_tile_rows(anomaly, field.shape)
     cells = TILES * LANES // lax.axis_size("year")
     share = lax.dynamic_slice(

time: 63 us -> 55.3 us (0.88)
  Pallas kernels: 57.3 us -> 52.2 us
  local copies, waits for them, and re-layouts: 4.45 us -> 0.89 us
  other arithmetic: 0 us -> 1.38 us
    pallas_call x1, Pallas kernels: 8.69 us -> 3.06 us  [anomaly_of(): pl.pallas_call(subtract_kernel, out_shape=jax.ShapeDtypeStruct((rows, LAN...]
    unnamed x6 -> x0, local copies, waits for them, and re-layouts: 3.56 us -> none
    select_n x0 -> x1, other arithmetic: none -> 0.69 us  [local(): counts = jnp.where(moved, -counts, counts)]
    ne x0 -> x1, other arithmetic: none -> 0.69 us  [local(): moved = (day_index != slot)[:, None, :]]
where the time goes in v2:
time: 55.3 us; the launch traced here: 55.1 us
  Pallas kernels  52.2 us (94%)
  other arithmetic  1.38 us (2%)
  local copies, waits for them, and re-layouts  0.89 us (2%)
  between operations  0.66 us (1%)
    pallas_call x1, Pallas kernels, climate_of(): pl.pallas_call(reduce_kernel, out_shape=(jax.ShapeDtypeStruct((ROWS, HOUR...  49.1 us
    pallas_call x1, Pallas kernels, anomaly_of(): pl.pallas_call(subtract_kernel, out_shape=jax.ShapeDtypeStruct((rows, LAN...  3.06 us

profile of v2, /device:TPU:0, one launch (start us, length us, event | category | flops | bytes accessed | tf_op | source)
XLA Modules:
  0.0 55.1 jit_solution(13293239616466192780)
XLA Ops:
  0.6 0.7 %broadcast_compare_fusion = pred[4,23]{1,0:T(4,128)(4,1)S(1)} fusion(s32[4,23]{1,0:T(4,128)} %param.4, s32[23]{0:T(128)S(1)} %iota_add_fusion), kind=kLoop, calls=%fused_computation.2 | loop fusion | flops 92 | bytes 552 | tf_op jit(solution)/shard_map/ne | solution.py:491
  1.3 0.7 %negate_select_fusion.count_ref = s32[4,2,23]{2,1,0:T(2,128)S(1)} fusion(s32[4,23,2]{1,2,0:T(2,128)} %param.5, pred[4,23]{1,0:T(4,128)(4,1)S(1)} %broadcast_compare_fusion), kind=kLoop, calls=%fused_computation.1 | loop fusion | flops 368 | bytes 1564 | tf_op jit(solution)/shard_map/jit(_where)/select_n | solution.py:493
  2.0 49.1 %climate.1 = (f32[24,2,11776]{2,1,0:T(2,128)S(1)}, bf16[4,23,2,11520]{3,2,1,0:T(2,128)(2,1)S(1)}) custom-call(bf16[4,23,2,11520]{3,2,1,0:T(2,128)(2,1)} %field.1, s32[4,2,23]{2,1,0:T(2,128)S(1)} %negate_select_fusion.count_ref), custom_call_target="tpu_custom_call" | custom-call | tf_op jit(solution)/shard_map/climate/pallas_call | solution.py:382
  51.1 3.1 %anomaly.1 = bf16[16560,128]{1,0:T(8,128)(2,1)} custom-call(s32[4,2,23]{2,1,0:T(2,128)S(1)} %negate_select_fusion.count_ref, bf16[16560,128]{1,0:T(8,128)(2,1)S(1)} %bitcast.17, f32[4416,128]{1,0:T(8,128)S(1)} %bitcast.18), custom_call_target="tpu_custom_call" | custom-call | tf_op jit(solution)/shard_map/anomaly/pallas_call | solution.py:454
  54.2 0.9 %dynamic-slice_convert_fusion = bf16[23,2,1440]{2,1,0:T(2,128)(2,1)} fusion(f32[24,2,11776]{2,1,0:T(2,128)S(1)} %get-tuple-element.5, s32[]{:T(128)S(6)} %select_n.8), kind=kLoop, calls=%fused_computation | loop fusion | bytes 264964 | tf_op jit(solution)/shard_map/convert_element_type | solution.py:501
  (1 shorter events, 0.0 us)

commit v3 on v2

v3 whole, which is shorter than its diff:
```python
import functools

import jax
import jax.numpy as jnp
from jax import lax
from jax.experimental import pallas as pl
from jax.experimental.layout import Layout, with_layout_constraint
from jax.experimental.pallas import tpu as pltpu
from jax.sharding import PartitionSpec as P

MESH = pl.DeviceIdType.MESH
HALF = 30
YEARS, DAYS, HOURS, TILES = 4, 23, 2, 90
LANES = 128
ROWS = DAYS + 1
MID = ROWS // 2
SLOT = 23
GROUPS = ((7, 6), (6, 4))
EDGE = ROWS // 3
MESSAGES = 8 + 44 * len(GROUPS)


def lanes(start, tiles):
    if isinstance(start, int):
        return pl.ds(start * LANES, tiles * LANES)
    return pl.ds(pl.multiple_of(start * LANES, LANES), tiles * LANES)


def rows_of(low):
    return pl.ds(0, MID) if low else pl.ds(MID, MID)


def shares(group):
    first, second = group
    return (first + 1) // 2, first // 2, second // 2


def reduce_kernel(
    field, count_ref, cl, held, part, weight, first_count, second_count,
    count0, count1, count2, count_x, count_z, count_d, kept, inverse, load_sem, send_sem, recv_sem,
    *buffers,
):
    day = lax.axis_index("day")
    year = lax.axis_index("year")
    days = lax.axis_size("day")
    z, u = year // 2, year % 2
    up, down, across = (z + 1) % 4, (z + 3) % 4, (z + 2) % 4
    at_up, at_down, at_across = (day, up * 2 + u), (day, down * 2 + u), (day, across * 2 + u)
    twin = (day, z * 2 + (1 - u))
    beside = [((day + step + days) % days, year) for step in (1, -1, 2, -2)]
    peers = [at_up, at_down, at_across, twin] + beside

    barrier = pltpu.get_barrier_semaphore()
    for peer in peers:
        pl.semaphore_signal(barrier, inc=1, device_id=peer, device_id_type=MESH)

    order = (across, up, down, z)
    inner = SLOT - 4 * SLOT + TILES
    loads = []
    for number, s in enumerate(order):
        span = lanes(s * SLOT, inner)
        loads.append((field.at[:, :, :, span], held.at[:, :, :, span], load_sem.at[number]))
    for s in range(3):
        span = lanes(s * SLOT + inner, SLOT - inner)
        loads.append((field.at[:, :, :, span], held.at[:, :, :, span], load_sem.at[4 + s]))
    loads = [pltpu.make_async_copy(*load) for load in loads]
    for load in loads[:1] + loads[4:] + loads[1:4]:
        load.start()

    used = []

    def copy(source, target, device):
        number = len(used)
        used.append(
            pltpu.make_async_remote_copy(
                src_ref=source, dst_ref=target, send_sem=send_sem.at[number],
                recv_sem=recv_sem.at[number], device_id=device, device_id_type=MESH,
            )
        )
        used[-1].start()
        return used[-1]

    total_own = jnp.zeros((HOURS, DAYS), jnp.float32)
    total_next = jnp.zeros((HOURS, DAYS), jnp.float32)
    for y in range(YEARS):
        counts = count_ref[y].astype(jnp.float32)
        own = jnp.maximum(counts, 0.0)
        after = jnp.maximum(-counts, 0.0)
        total_own += own
        total_next += after
        for s in range(DAYS):
            weight[y, s] = jnp.broadcast_to(own[:, s : s + 1], (HOURS, 4 * LANES))
            weight[y, DAYS + s] = jnp.broadcast_to(after[:, s : s + 1], (HOURS, 4 * LANES))
    first_count[...] = jnp.zeros_like(first_count)
    second_count[...] = jnp.zeros_like(second_count)
    first_count[:, :DAYS] = total_own
    second_count[:, :DAYS] = total_next
    count0[...] = first_count[...] + pltpu.roll(second_count[...], 1, 1)

    def add_years(start, tiles):
        halves = [(h, min(4, tiles - h)) for h in range(0, tiles, 4)]
        carried = [None] * len(halves)
        for s in range(DAYS):
            own = [None] * len(halves)
            after = [None] * len(halves)
            for y in range(YEARS):
                value = held[y, s, :, lanes(start, tiles)].astype(jnp.float32)
                for n, (h, width) in enumerate(halves):
                    piece = value[:, h * LANES : (h + width) * LANES]
                    a = piece * weight[y, s, :, : width * LANES]
                    b = piece * weight[y, DAYS + s, :, : width * LANES]
                    own[n] = a if y == 0 else own[n] + a
                    after[n] = b if y == 0 else after[n] + b
            for n, (h, width) in enumerate(halves):
                row = own[n] if s == 0 else own[n] + carried[n]
                part[s, :, lanes(start + h, width)] = row
            carried = after
        for n, (h, width) in enumerate(halves):
            part[DAYS, :, lanes(start + h, width)] = carried[n]

    part[:, :, TILES * LANES :] = jnp.zeros((ROWS, HOURS, (4 * SLOT - TILES) * LANES), jnp.float32)
    added = []

    def ready(number):
        while len(added) <= number:
            s = order[len(added)]
            for load in loads[:1] + loads[4:] if not added else loads[len(added) : len(added) + 1]:
                load.wait()
            start = s * SLOT

            @pl.loop(0, inner // 8)
            def _(step):
                add_years(start + step * 8, 8)

            add_years(start + inner // 8 * 8, inner % 8)

            @pl.when(s < 3)
            def _():
                add_years(start + inner, SLOT - inner)

            added.append(s)

    ready(0)
    pl.semaphore_wait(barrier, len(peers))

    class Ring:
        def __init__(self, buffers, at, tiles):
            self.buffers, self.at, self.tiles = buffers, at, tiles

        def piece(self, low, s):
            return part.at[rows_of(low), :, lanes(self.at(s), self.tiles)]

        def begin(self):
            ready(0)
            self.far_up = copy(self.piece(True, across), self.buffers.at[0], at_up)
            self.far_down = copy(self.piece(False, across), self.buffers.at[1], at_down)

        def near_up(self):
            ready(1)
            self.up = copy(self.piece(False, up), self.buffers.at[2], at_up)

        def near_down(self):
            ready(2)
            self.down = copy(self.piece(True, down), self.buffers.at[3], at_down)

        def forward(self):
            ready(2)
            self.far_up.wait_recv()
            self.add(True, up, 0)
            self.on_up = copy(self.piece(True, up), self.buffers.at[4], at_up)
            self.far_down.wait_recv()
            self.add(False, down, 1)
            self.on_down = copy(self.piece(False, down), self.buffers.at[5], at_down)

        def add(self, low, s, number):
            where = (rows_of(low), slice(None), lanes(self.at(s), self.tiles))
            part[where] = part[where] + self.buffers[number]

        def result(self):
            ready(3)
            self.up.wait_recv()
            self.down.wait_recv()
            self.on_up.wait_recv()
            self.on_down.wait_recv()
            where = lanes(self.at(z), self.tiles)
            low = part[rows_of(True), :, where] + self.buffers[3] + self.buffers[4]
            high = part[rows_of(False), :, where] + self.buffers[2] + self.buffers[5]
            return low, high

    class Spread:
        def __init__(self, at, tiles):
            self.at, self.tiles = at, tiles

        def send(self, low, s, device):
            piece = cl.at[rows_of(low), :, lanes(self.at(s), self.tiles)]
            return copy(piece, piece, device)

        def begin(self):
            self.up0 = self.send(True, z, at_up)
            self.down0 = self.send(False, z, at_down)
            self.up1 = self.send(False, z, at_up)
            self.down1 = self.send(True, z, at_down)

        def forward(self):
            self.up0.wait_recv()
            self.up2 = self.send(True, down, at_up)
            self.down0.wait_recv()
            self.down2 = self.send(False, up, at_down)

        def near(self):
            self.up1.wait_recv()
            self.down1.wait_recv()

        def far(self):
            self.up2.wait_recv()
            self.down2.wait_recv()

    class Group:
        def __init__(self, number):
            self.first, self.second = GROUPS[number]
            start = sum(map(sum, GROUPS[:number]))
            self.share, self.stride, self.half = shares(GROUPS[number])
            first_in, second_in, self.second_x, self.first_x, self.own, self.window = buffers[
                6 * number : 6 * number + 6
            ]
            self.first_at = lambda s: s * SLOT + start
            self.second_at = lambda s: s * SLOT + start + self.first
            self.kept_at = lambda s: self.second_at(s) + u * self.half
            self.ring = Ring(first_in, self.first_at, self.first)
            self.late_ring = Ring(second_in, self.kept_at, self.half)
            self.own_spread = Spread(lambda s: self.first_at(s) + u * self.stride, self.share)
            self.other_spread = Spread(
                lambda s: self.first_at(s) + (1 - u) * self.share, self.stride
            )
            self.late_spread = Spread(self.kept_at, self.half)
            self.swaps = []
            self.last = []

        def swap(self, *numbers):
            for number in numbers:
                ready(number)
                start = self.second_at(order[number]) + (1 - u) * self.half
                source = part.at[:, :, lanes(start, self.half)]
                self.swaps.append(copy(source, self.second_x.at[number], twin))

        def swapped(self, number):
            self.swaps[number].wait_recv()
            where = (slice(None), slice(None), lanes(self.kept_at(order[number]), self.half))
            part[where] = part[where] + self.second_x[number]

        def near(self):
            self.ring.near_up()
            self.ring.near_down()

        def late_begin(self):
            self.swapped(0)
            self.late_ring.begin()

        def late_near(self):
            self.swapped(1)
            self.late_ring.near_up()
            self.swapped(2)
            self.late_ring.near_down()

        def swap_first(self):
            low, high = self.ring.result()
            where = lanes(self.first_at(z), self.first)
            part[rows_of(True), :, where] = low
            part[rows_of(False), :, where] = high
            start = self.first_at(z) + (1 - u) * self.stride
            self.pair = copy(part.at[:, :, lanes(start, self.share)], self.first_x, twin)

        def late_result(self):
            self.swapped(3)
            low, high = self.late_ring.result()
            span = pl.ds(self.share * LANES, self.half * LANES)
            self.own[rows_of(True), :, span] = low
            self.own[rows_of(False), :, span] = high

        def share_out(self):
            self.pair.wait_recv()
            span = lanes(self.first_at(z) + u * self.stride, self.share)
            self.own[:, :, : self.share * LANES] = part[:, :, span] + self.first_x[...]
            right, left, right2, left2 = beside
            own, window = self.own, self.window
            self.out = [
                copy(own, window.at[pl.ds(0, ROWS)], right),
                copy(own, window.at[pl.ds(ROWS, ROWS)], left),
                copy(own.at[pl.ds(ROWS - EDGE, EDGE)], window.at[pl.ds(2 * ROWS, EDGE)], right2),
                copy(own.at[pl.ds(0, EDGE)], window.at[pl.ds(2 * ROWS + EDGE, EDGE)], left2),
            ]

        def smooth(self):
            for message in self.out:
                message.wait_recv()
            own, window = self.own, self.window

            def day_row(offset, span):
                if offset < -DAYS:
                    return window[2 * ROWS + offset + 2 * DAYS - (ROWS - EDGE), :, span]
                if offset == -DAYS:
                    return window[0, :, span] + window[2 * ROWS + EDGE - 1, :, span]
                if offset < 0:
                    return window[offset + DAYS, :, span]
                if offset == 0:
                    return own[0, :, span] + window[DAYS, :, span]
                if offset < DAYS:
                    return own[offset, :, span]
                if offset == DAYS:
                    return window[ROWS, :, span] + own[DAYS, :, span]
                if offset < 2 * DAYS:
                    return window[ROWS + offset - DAYS, :, span]
                if offset == 2 * DAYS:
                    return window[2 * ROWS + EDGE, :, span] + window[ROWS + DAYS, :, span]
                return window[2 * ROWS + EDGE + offset - 2 * DAYS, :, span]

            def smoothed(start, at, tiles):
                for h in range(0, tiles, 4):
                    width = min(4, tiles - h)
                    span = pl.ds((start + h) * LANES, width * LANES)
                    total = day_row(0, span)
                    for offset in range(1, DAYS):
                        total = total + day_row(offset, span)
                    for offset in range(-1, -HALF - 1, -1):
                        total = total + day_row(offset, span)
                        if offset + HALF < ROWS:
                            kept[offset + HALF, :, : width * LANES] = total
                    total = None
                    for offset in range(DAYS, DAYS + HALF + 1):
                        row = day_row(offset, span)
                        total = row if total is None else total + row
                        if offset >= HALF:
                            i = offset - HALF
                            sums = kept[i, :, : width * LANES] + total
                            scaled = sums * inverse[i, :, : width * LANES]
                            cl[i, :, lanes(at + h, width)] = scaled

            smoothed(0, self.first_at(z) + u * self.stride, self.share)
            smoothed(self.share, self.kept_at(z), self.half)

        def across_x(self, s):
            piece = cl.at[:, :, lanes(self.kept_at(s), self.half)]
            self.last.append(copy(piece, piece, twin))

        def spread_second(self):
            self.late_spread.begin()
            self.across_x(z)

        def spread_first(self):
            piece = cl.at[:, :, lanes(self.first_at(z) + u * self.share, self.stride)]
            self.pair = copy(piece, piece, twin)
            self.own_spread.begin()

        def late_forward(self):
            self.late_spread.forward()

        def late_across(self):
            self.late_spread.near()
            self.across_x(up)
            self.across_x(down)

        def other(self):
            self.pair.wait_recv()
            self.other_spread.begin()

        def late_far(self):
            self.late_spread.far()
            self.across_x(across)

        def end(self):
            for portion in (self.own_spread, self.other_spread):
                portion.near()
                portion.far()
            for message in self.last:
                message.wait_recv()

    def windows():
        for message in aside:
            message.wait_recv()
        spread = (
            count_d[2]
            + pltpu.roll(count_d[0], DAYS, 1)
            + pltpu.roll(count2[...], 2 * DAYS, 1)
            + pltpu.roll(count_d[1], 3 * DAYS, 1)
            + pltpu.roll(count_d[3], 4 * DAYS, 1)
        )
        lane = lax.broadcasted_iota(jnp.int32, (HOURS, LANES), 1)
        for i in range(ROWS):
            start = 2 * DAYS - HALF + i
            inside = (lane >= start) & (lane <= start + 2 * HALF)
            count = jnp.sum(jnp.where(inside, spread, 0.0), axis=1, keepdims=True)
            inverse[i] = jnp.broadcast_to(1.0 / count, (HOURS, 4 * LANES))

    send_count = copy(count0, count_x, twin)
    one, two = (Group(number) for number in range(len(GROUPS)))
    one.ring.begin()
    two.swap(0)
    one.swap(0)
    two.swap(1)
    one.swap(1, 2)
    two.ring.begin()
    two.swap(2)
    one.near()
    send_count.wait_recv()
    count1[...] = count0[...] + count_x[...]
    along = [copy(count1, count_z.at[n], d) for n, d in enumerate((at_up, at_down, at_across))]
    one.ring.forward()
    one.late_begin()
    two.ring.forward()
    one.swap(3)
    two.near()
    one.swap_first()
    one.late_near()
    two.swap(3)
    one.late_ring.forward()
    two.late_begin()
    two.swap_first()
    one.late_result()
    two.late_near()
    for message in along:
        message.wait_recv()
    count2[...] = count1[...] + count_z[0] + count_z[1] + count_z[2]
    aside = [copy(count2, count_d.at[n], d) for n, d in enumerate(beside)]
    one.share_out()
    two.late_ring.forward()
    two.late_result()
    two.share_out()
    windows()
    one.smooth()
    one.spread_second()
    one.spread_first()
    two.smooth()
    two.spread_second()
    one.late_forward()
    two.spread_first()
    one.late_across()
    two.late_forward()
    two.late_across()
    one.other()
    one.late_far()
    two.own_spread.forward()
    two.other()
    two.late_far()
    one.own_spread.forward()
    one.other_spread.forward()
    two.other_spread.forward()
    for group in (one, two):
        group.end()
    for message in used:
        message.wait_send()


def climate_of(field, counts):
    f32 = jnp.float32
    wide = 4 * SLOT * LANES
    vmem = pltpu.VMEM
    row = (HOURS, LANES)
    scratch = [
        vmem((ROWS, HOURS, wide), f32),
        vmem((YEARS, 2 * DAYS, HOURS, 4 * LANES), f32),
        vmem(row, f32), vmem(row, f32), vmem(row, f32), vmem(row, f32), vmem(row, f32),
        vmem(row, f32), vmem((3, *row), f32), vmem((4, *row), f32),
        vmem((ROWS, HOURS, 4 * LANES), f32),
        vmem((ROWS, HOURS, 4 * LANES), f32),
        pltpu.SemaphoreType.DMA((7,)),
        pltpu.SemaphoreType.DMA((MESSAGES,)),
        pltpu.SemaphoreType.DMA((MESSAGES,)),
    ]
    for group in GROUPS:
        share, _, half = shares(group)
        together = (share + half) * LANES
        scratch += [
            vmem((6, MID, HOURS, group[0] * LANES), f32),
            vmem((6, MID, HOURS, half * LANES), f32),
            vmem((4, ROWS, HOURS, half * LANES), f32),
            vmem((ROWS, HOURS, share * LANES), f32),
            vmem((ROWS, HOURS, together), f32),
            vmem((2 * ROWS + 2 * EDGE, HOURS, together), f32),
        ]
    return pl.pallas_call(
        reduce_kernel,
        out_shape=(
            jax.ShapeDtypeStruct((ROWS, HOURS, wide), f32),
            jax.ShapeDtypeStruct(field.shape, field.dtype),
        ),
        in_specs=[
            pl.BlockSpec(memory_space=pltpu.HBM),
            pl.BlockSpec(memory_space=vmem),
        ],
        out_specs=[pl.BlockSpec(memory_space=vmem)] * 2,
        scratch_shapes=scratch,
        compiler_params=pltpu.CompilerParams(
            collective_id=0, has_side_effects=True, vmem_limit_bytes=46 * 2**20
        ),
        name="climate",
    )(field, counts)


STRIP = HOURS * TILES
WIDE = HOURS * 4 * SLOT
PAIRS = YEARS * DAYS // 2
GROUP = 2


def subtract_kernel(count_ref, field, climate, out, moved_on, ready, store_sem):
    size = GROUP * 2 * STRIP
    groups = PAIRS // GROUP

    @pl.loop(0, ROWS)
    def _(e):
        base = pl.multiple_of(e * (WIDE + 8), 8)
        value = climate[pl.ds(pl.multiple_of(e * WIDE, 8), STRIP), :]
        moved_on[pl.ds(base + 4, STRIP), :] = value

    sublane = lax.broadcasted_iota(jnp.int32, (8, LANES), 0)

    def row_of(k):
        y, s = divmod(k, DAYS)
        ahead = (count_ref[y, 0, s] < 0).astype(jnp.int32)
        return s + ahead

    stores = []
    body = STRIP - STRIP % 8
    for g in range(groups):
        for pair in range(g * GROUP, (g + 1) * GROUP):
            start = pair * 2 * STRIP
            even = pl.multiple_of(row_of(2 * pair) * WIDE, 8)
            odd = pl.multiple_of(row_of(2 * pair + 1) * (WIDE + 8), 8)

            def put(offset, size, value):
                span = pl.ds(start + offset, size)
                ready[span, :] = (field[span, :].astype(jnp.float32) - value).astype(jnp.bfloat16)

            put(0, body, climate[pl.ds(even, body), :])
            middle = jnp.where(
                sublane < 4, climate[pl.ds(even + body, 8), :], moved_on[pl.ds(odd, 8), :]
            )
            put(body, 8, middle)
            put(body + 8, body, moved_on[pl.ds(odd + 8, body), :])
        store = pltpu.make_async_copy(
            ready.at[pl.ds(g * size, size)], out.at[pl.ds(g * size, size)], store_sem.at[g]
        )
        store.start()
        stores.append(store)
    for store in stores:
        store.wait()


def anomaly_of(field, counts, climate):
    rows = YEARS * DAYS * STRIP
    groups = PAIRS // GROUP
    return pl.pallas_call(
        subtract_kernel,
        out_shape=jax.ShapeDtypeStruct((rows, LANES), jnp.bfloat16),
        in_specs=[
            pl.BlockSpec(memory_space=pltpu.SMEM),
            pl.BlockSpec(memory_space=pltpu.VMEM),
            pl.BlockSpec(memory_space=pltpu.VMEM),
        ],
        out_specs=pl.BlockSpec(memory_space=pltpu.HBM),
        scratch_shapes=[
            pltpu.VMEM((ROWS * (WIDE + 8), LANES), jnp.float32),
            pltpu.VMEM((rows, LANES), jnp.bfloat16),
            pltpu.SemaphoreType.DMA((groups,)),
        ],
        compiler_params=pltpu.CompilerParams(vmem_limit_bytes=40 * 2**20),
        name="anomaly",
    )(counts, field, climate)


def tile_rows(array):
    *lead, hours, cells = array.shape
    tiles = cells // LANES
    split = array.reshape(-1, hours, tiles, LANES)
    split = with_layout_constraint(split, Layout(major_to_minor=(0, 2, 1, 3)))
    return split.transpose(0, 2, 1, 3).reshape(-1, LANES)


def from_tile_rows(rows, shape):
    *lead, hours, cells = shape
    tiles = cells // LANES
    split = rows.reshape(-1, tiles, hours, LANES).transpose(0, 2, 1, 3)
    split = with_layout_constraint(split, Layout(major_to_minor=(0, 2, 1, 3)))
    return split.reshape(shape)


def local(field, day_index, sample_count):
    slot = lax.broadcasted_iota(jnp.int32, sample_count.shape, 1) + lax.axis_index("day") * DAYS
    counts = jnp.where(day_index[:, :, None] != slot, -sample_count, sample_count)
    counts = jnp.transpose(counts, (0, 2, 1))
    climate, field = climate_of(field, counts)
    anomaly = anomaly_of(tile_rows(field), counts, tile_rows(climate))
    anomaly = from_tile_rows(anomaly, field.shape)
    cells = TILES * LANES // lax.axis_size("year")
    share = lax.dynamic_slice(
        climate, (0, 0, lax.axis_index("year") * cells), (DAYS, HOURS, cells)
    )
    return anomaly, share.astype(jnp.bfloat16)


def solution(mesh):
    return jax.shard_map(
        local,
        mesh=mesh,
        in_specs=(P("year", "day", None, None), P("year", "day"), P("year", "day", None)),
        out_specs=(P("year", "day", None, None), P("day", None, "year")),
        check_vma=False,
    )
```

time: 55.3 us -> 52.7 us (0.953); the launches traced: 55.1 us -> 51.9 us
  Pallas kernels: 52.2 us -> 49.6 us
  other arithmetic: 1.38 us -> 0.71 us
    pallas_call x1, Pallas kernels: 49.1 us -> 46.6 us  [climate_of(): pl.pallas_call(reduce_kernel, out_shape=(jax.ShapeDtypeStruct((ROWS, HOUR...]
    transpose x0 -> x1, other arithmetic: none -> 0.71 us  [local(): counts = jnp.transpose(counts, (0, 2, 1))]
    select_n x1 -> x0, other arithmetic: 0.69 us -> none  [local(): counts = jnp.where(moved, -counts, counts)]
    ne x1 -> x0, other arithmetic: 0.69 us -> none  [local(): moved = (day_index != slot)[:, None, :]]
where the time goes in v3:
time: 52.7 us; the launch traced here: 51.9 us
  Pallas kernels  49.6 us (94%)
  local copies, waits for them, and re-layouts  0.89 us (2%)
  other arithmetic  0.71 us (1%)
  between operations  0.66 us (1%)
    pallas_call x1, Pallas kernels, climate_of(): pl.pallas_call(reduce_kernel, out_shape=(jax.ShapeDtypeStruct((ROWS, HOUR...  46.6 us
    pallas_call x1, Pallas kernels, anomaly_of(): pl.pallas_call(subtract_kernel, out_shape=jax.ShapeDtypeStruct((rows, LAN...  3.06 us

profile of v3, /device:TPU:0, one launch (start us, length us, event | category | flops | bytes accessed | tf_op | source)
XLA Modules:
  0.0 51.9 jit_solution(11533503153339635108)
XLA Ops:
  0.6 0.7 %fusion.count_ref = s32[4,2,23]{2,1,0:T(2,128)S(1)} fusion(s32[4,23,2]{1,2,0:T(2,128)} %param.5, s32[23]{0:T(128)S(1)} %iota_add_fusion, s32[4,23]{1,0:T(4,128)} %param.4), kind=kLoop, calls=%fused_computation.2 | loop fusion | flops 552 | bytes 1932 | tf_op jit(solution)/shard_map/transpose | solution.py:590
  1.4 46.6 %climate.1 = (f32[24,2,11776]{2,1,0:T(2,128)S(1)}, bf16[4,23,2,11520]{3,2,1,0:T(2,128)(2,1)S(1)}) custom-call(bf16[4,23,2,11520]{3,2,1,0:T(2,128)(2,1)} %field.1, s32[4,2,23]{2,1,0:T(2,128)S(1)} %fusion.count_ref), custom_call_target="tpu_custom_call" | custom-call | tf_op jit(solution)/shard_map/climate/pallas_call | solution.py:480
  47.9 3.1 %anomaly.1 = bf16[16560,128]{1,0:T(8,128)(2,1)} custom-call(s32[4,2,23]{2,1,0:T(2,128)S(1)} %fusion.count_ref, bf16[16560,128]{1,0:T(8,128)(2,1)S(1)} %bitcast.17, f32[4416,128]{1,0:T(8,128)S(1)} %bitcast.18), custom_call_target="tpu_custom_call" | custom-call | tf_op jit(solution)/shard_map/anomaly/pallas_call | solution.py:552
  51.0 0.9 %dynamic-slice_convert_fusion = bf16[23,2,1440]{2,1,0:T(2,128)(2,1)} fusion(f32[24,2,11776]{2,1,0:T(2,128)S(1)} %get-tuple-element.5, s32[]{:T(128)S(6)} %select_n.8), kind=kLoop, calls=%fused_computation | loop fusion | bytes 264964 | tf_op jit(solution)/shard_map/convert_element_type | solution.py:598
  (1 shorter events, 0.0 us)

commit v4 on v3

--- a/solution.py
+++ b/solution.py
@@ -502,30 +502,38 @@
 GROUP = 2
 
 
-def subtract_kernel(count_ref, field, climate, out, moved_on, ready, store_sem):
+def subtract_kernel(count_ref, field, climate, by_hour, out, share, ready, cut, store_sem):
     size = GROUP * 2 * STRIP
     groups = PAIRS // GROUP
-
-    @pl.loop(0, ROWS)
-    def _(e):
-        base = pl.multiple_of(e * (WIDE + 8), 8)
-        value = climate[pl.ds(pl.multiple_of(e * WIDE, 8), STRIP), :]
-        moved_on[pl.ds(base + 4, STRIP), :] = value
-
     sublane = lax.broadcasted_iota(jnp.int32, (8, LANES), 0)
 
     def row_of(k):
         y, s = divmod(k, DAYS)
         ahead = (count_ref[y, 0, s] < 0).astype(jnp.int32)
-        return s + ahead
+        return pl.multiple_of((s + ahead) * WIDE, 8)
+
+    def cut_share():
+        year = lax.axis_index("year")
+        cells = share.shape[2]
+        tiles = pl.cdiv(cells, LANES)
+        part = cells % LANES
+        for quarter in range(LANES // part):
+
+            @pl.when(year % (LANES // part) == quarter)
+            def _():
+                start = year * cells - quarter * part
+                span = pl.ds(pl.multiple_of(start, LANES), tiles * LANES)
+                for e in range(DAYS):
+                    row = by_hour[e, :, span]
+                    cut[e] = row[:, quarter * part : quarter * part + cells].astype(jnp.bfloat16)
 
     stores = []
     body = STRIP - STRIP % 8
     for g in range(groups):
         for pair in range(g * GROUP, (g + 1) * GROUP):
             start = pair * 2 * STRIP
-            even = pl.multiple_of(row_of(2 * pair) * WIDE, 8)
-            odd = pl.multiple_of(row_of(2 * pair + 1) * (WIDE + 8), 8)
+            even = row_of(2 * pair)
+            odd = row_of(2 * pair + 1)
 
             def put(offset, size, value):
                 span = pl.ds(start + offset, size)
@@ -533,39 +541,46 @@
 
             put(0, body, climate[pl.ds(even, body), :])
             middle = jnp.where(
-                sublane < 4, climate[pl.ds(even + body, 8), :], moved_on[pl.ds(odd, 8), :]
+                sublane < 4,
+                climate[pl.ds(even + body, 8), :],
+                pltpu.roll(climate[pl.ds(odd, 8), :], 4, 0),
             )
             put(body, 8, middle)
-            put(body + 8, body, moved_on[pl.ds(odd + 8, body), :])
+            put(body + 8, body, climate[pl.ds(odd + 4, body), :])
         store = pltpu.make_async_copy(
             ready.at[pl.ds(g * size, size)], out.at[pl.ds(g * size, size)], store_sem.at[g]
         )
         store.start()
         stores.append(store)
+        if g == groups // 2:
+            cut_share()
+            stores.append(pltpu.make_async_copy(cut, share, store_sem.at[groups]))
+            stores[-1].start()
     for store in stores:
         store.wait()
 
 
-def anomaly_of(field, counts, climate):
+def anomaly_of(field, counts, climate, cells):
     rows = YEARS * DAYS * STRIP
     groups = PAIRS // GROUP
+    share = (DAYS, HOURS, cells)
+    vmem = pl.BlockSpec(memory_space=pltpu.VMEM)
     return pl.pallas_call(
         subtract_kernel,
-        out_shape=jax.ShapeDtypeStruct((rows, LANES), jnp.bfloat16),
-        in_specs=[
-            pl.BlockSpec(memory_space=pltpu.SMEM),
-            pl.BlockSpec(memory_space=pltpu.VMEM),
-            pl.BlockSpec(memory_space=pltpu.VMEM),
-        ],
-        out_specs=pl.BlockSpec(memory_space=pltpu.HBM),
+        out_shape=(
+            jax.ShapeDtypeStruct((rows, LANES), jnp.bfloat16),
+            jax.ShapeDtypeStruct(share, jnp.bfloat16),
+        ),
+        in_specs=[pl.BlockSpec(memory_space=pltpu.SMEM), vmem, vmem, vmem],
+        out_specs=[pl.BlockSpec(memory_space=pltpu.HBM)] * 2,
         scratch_shapes=[
-            pltpu.VMEM((ROWS * (WIDE + 8), LANES), jnp.float32),
             pltpu.VMEM((rows, LANES), jnp.bfloat16),
-            pltpu.SemaphoreType.DMA((groups,)),
+            pltpu.VMEM(share, jnp.bfloat16),
+            pltpu.SemaphoreType.DMA((groups + 1,)),
         ],
         compiler_params=pltpu.CompilerParams(vmem_limit_bytes=40 * 2**20),
         name="anomaly",
-    )(counts, field, climate)
+    )(counts, tile_rows(field), tile_rows(climate), climate)
 
 
 def tile_rows(array):
@@ -589,13 +604,9 @@
     counts = jnp.where(day_index[:, :, None] != slot, -sample_count, sample_count)
     counts = jnp.transpose(counts, (0, 2, 1))
     climate, field = climate_of(field, counts)
-    anomaly = anomaly_of(tile_rows(field), counts, tile_rows(climate))
-    anomaly = from_tile_rows(anomaly, field.shape)
     cells = TILES * LANES // lax.axis_size("year")
-    share = lax.dynamic_slice(
-        climate, (0, 0, lax.axis_index("year") * cells), (DAYS, HOURS, cells)
-    )
-    return anomaly, share.astype(jnp.bfloat16)
+    anomaly, share = anomaly_of(field, counts, climate, cells)
+    return from_tile_rows(anomaly, field.shape), share
 
 
 def solution(mesh):

time: 52.7 us -> 51.6 us (0.979)
  local copies, waits for them, and re-layouts: 0.89 us -> 0 us
    convert_element_type x1 -> x0, local copies, waits for them, and re-layouts: 0.89 us -> none  [local(): return (anomaly, share.astype(jnp.bfloat16))]
where the time goes in v4:
time: 51.6 us; the launch traced here: 50.8 us
  Pallas kernels  49.5 us (96%)
  other arithmetic  0.71 us (1%)
  between operations  0.65 us (1%)
    pallas_call x1, Pallas kernels, climate_of(): pl.pallas_call(reduce_kernel, out_shape=(jax.ShapeDtypeStruct((ROWS, HOUR...  46.6 us
    pallas_call x1, Pallas kernels, anomaly_of(): pl.pallas_call(subtract_kernel, out_shape=(jax.ShapeDtypeStruct((rows, LA...  2.91 us

profile of v4, /device:TPU:0, one launch (start us, length us, event | category | flops | bytes accessed | tf_op | source)
XLA Modules:
  0.0 50.8 jit_solution(10674356072494892801)
XLA Ops:
  0.6 0.7 %fusion.count_ref = s32[4,2,23]{2,1,0:T(2,128)S(1)} fusion(s32[4,23,2]{1,2,0:T(2,128)} %param.5, s32[23]{0:T(128)S(1)} %iota_add_fusion, s32[4,23]{1,0:T(4,128)} %param.4), kind=kLoop, calls=%fused_computation.1 | loop fusion | flops 552 | bytes 1932 | tf_op jit(solution)/shard_map/transpose | solution.py:605
  1.4 46.6 %climate.1 = (f32[24,2,11776]{2,1,0:T(2,128)S(1)}, bf16[4,23,2,11520]{3,2,1,0:T(2,128)(2,1)S(1)}) custom-call(bf16[4,23,2,11520]{3,2,1,0:T(2,128)(2,1)} %field.1, s32[4,2,23]{2,1,0:T(2,128)S(1)} %fusion.count_ref), custom_call_target="tpu_custom_call" | custom-call | tf_op jit(solution)/shard_map/climate/pallas_call | solution.py:480
  47.9 2.9 %anomaly.1 = (bf16[16560,128]{1,0:T(8,128)(2,1)}, bf16[23,2,1440]{2,1,0:T(2,128)(2,1)}) custom-call(s32[4,2,23]{2,1,0:T(2,128)S(1)} %fusion.count_ref, bf16[16560,128]{1,0:T(8,128)(2,1)S(1)} %bitcast.18, f32[4416,128]{1,0:T(8,128)S(1)} %bitcast.17, f32[24,2,11776]{2,1,0:T(2,128)S(1)} %get-tuple-element.7.by_hour), custom_call_target="tpu_custom_call" | custom-call | tf_op jit(solution)/shard_map/anomaly/pallas_call | solution.py:568
  (1 shorter events, 0.0 us)

commit v5 on v4

--- a/solution.py
+++ b/solution.py
@@ -15,7 +15,7 @@
 ROWS = DAYS + 1
 MID = ROWS // 2
 SLOT = 23
-GROUPS = ((7, 6), (6, 4))
+GROUPS = ((7, 4), (6, 6))
 EDGE = ROWS // 3
 MESSAGES = 8 + 44 * len(GROUPS)
 
@@ -176,6 +176,21 @@
             where = (rows_of(low), slice(None), lanes(self.at(s), self.tiles))
             part[where] = part[where] + self.buffers[number]
 
+        def straight(self):
+            ready(2)
+            self.far_up = copy(self.piece(True, across), self.buffers.at[0], at_across)
+            self.far_down = copy(self.piece(False, across), self.buffers.at[1], at_across)
+            self.up = copy(self.piece(False, up), self.buffers.at[2], at_up)
+            self.down = copy(self.piece(True, down), self.buffers.at[3], at_down)
+            self.on_up = copy(self.piece(True, up), self.buffers.at[4], at_up)
+            self.on_down = copy(self.piece(False, down), self.buffers.at[5], at_down)
+
+        def straight_result(self):
+            self.far_up.wait_recv()
+            self.far_down.wait_recv()
+            low, high = self.result()
+            return low + self.buffers[0], high + self.buffers[1]
+
         def result(self):
             ready(3)
             self.up.wait_recv()
@@ -189,19 +204,23 @@
 
     class Spread:
         def __init__(self, at, tiles):
-            self.at, self.tiles = at, tiles
+            self.at, self.tiles, self.forwarded = at, tiles, False
 
         def send(self, low, s, device):
             piece = cl.at[rows_of(low), :, lanes(self.at(s), self.tiles)]
             return copy(piece, piece, device)
 
-        def begin(self):
+        def begin(self, straight=False):
+            if straight:
+                self.up2 = self.send(True, z, at_across)
+                self.down2 = self.send(False, z, at_across)
             self.up0 = self.send(True, z, at_up)
             self.down0 = self.send(False, z, at_down)
             self.up1 = self.send(False, z, at_up)
             self.down1 = self.send(True, z, at_down)
 
         def forward(self):
+            self.forwarded = True
             self.up0.wait_recv()
             self.up2 = self.send(True, down, at_up)
             self.down0.wait_recv()
@@ -210,6 +229,12 @@
         def near(self):
             self.up1.wait_recv()
             self.down1.wait_recv()
+
+        def near_all(self):
+            if not self.forwarded:
+                self.up0.wait_recv()
+                self.down0.wait_recv()
+            self.near()
 
         def far(self):
             self.up2.wait_recv()
@@ -256,6 +281,11 @@
             self.swapped(0)
             self.late_ring.begin()
 
+        def late_straight(self):
+            for number in range(3):
+                self.swapped(number)
+            self.late_ring.straight()
+
         def late_near(self):
             self.swapped(1)
             self.late_ring.near_up()
@@ -270,9 +300,9 @@
             start = self.first_at(z) + (1 - u) * self.stride
             self.pair = copy(part.at[:, :, lanes(start, self.share)], self.first_x, twin)
 
-        def late_result(self):
+        def late_result(self, straight=False):
             self.swapped(3)
-            low, high = self.late_ring.result()
+            low, high = self.late_ring.straight_result() if straight else self.late_ring.result()
             span = pl.ds(self.share * LANES, self.half * LANES)
             self.own[rows_of(True), :, span] = low
             self.own[rows_of(False), :, span] = high
@@ -342,8 +372,8 @@
             piece = cl.at[:, :, lanes(self.kept_at(s), self.half)]
             self.last.append(copy(piece, piece, twin))
 
-        def spread_second(self):
-            self.late_spread.begin()
+        def spread_second(self, straight=False):
+            self.late_spread.begin(straight)
             self.across_x(z)
 
         def spread_first(self):
@@ -359,9 +389,9 @@
             self.across_x(up)
             self.across_x(down)
 
-        def other(self):
+        def other(self, straight=False):
             self.pair.wait_recv()
-            self.other_spread.begin()
+            self.other_spread.begin(straight)
 
         def late_far(self):
             self.late_spread.far()
@@ -369,7 +399,7 @@
 
         def end(self):
             for portion in (self.own_spread, self.other_spread):
-                portion.near()
+                portion.near_all()
                 portion.far()
             for message in self.last:
                 message.wait_recv()
@@ -439,11 +469,10 @@
     one.other()
     one.late_far()
     two.own_spread.forward()
-    two.other()
+    two.other(straight=True)
     two.late_far()
     one.own_spread.forward()
     one.other_spread.forward()
-    two.other_spread.forward()
     for group in (one, two):
         group.end()
     for message in used:

time: 51.6 us -> 51.2 us (level); the launches traced: 50.8 us -> 51 us
  no operation moved by 1% of the time
where the time goes in v5:
time: 51.2 us; the launch traced here: 51 us
  Pallas kernels  49.7 us (97%)
  other arithmetic  0.71 us (1%)
  between operations  0.65 us (1%)
    pallas_call x1, Pallas kernels, climate_of(): pl.pallas_call(reduce_kernel, out_shape=(jax.ShapeDtypeStruct((ROWS, HOUR...  46.8 us
    pallas_call x1, Pallas kernels, anomaly_of(): pl.pallas_call(subtract_kernel, out_shape=(jax.ShapeDtypeStruct((rows, LA...  2.91 us

profile of v5, /device:TPU:0, one launch (start us, length us, event | category | flops | bytes accessed | tf_op | source)
XLA Modules:
  0.0 51.0 jit_solution(10559370857841462704)
XLA Ops:
  0.6 0.7 %fusion.count_ref = s32[4,2,23]{2,1,0:T(2,128)S(1)} fusion(s32[4,23,2]{1,2,0:T(2,128)} %param.5, s32[23]{0:T(128)S(1)} %iota_add_fusion, s32[4,23]{1,0:T(4,128)} %param.4), kind=kLoop, calls=%fused_computation.1 | loop fusion | flops 552 | bytes 1932 | tf_op jit(solution)/shard_map/transpose | solution.py:634
  1.4 46.8 %climate.1 = (f32[24,2,11776]{2,1,0:T(2,128)S(1)}, bf16[4,23,2,11520]{3,2,1,0:T(2,128)(2,1)S(1)}) custom-call(bf16[4,23,2,11520]{3,2,1,0:T(2,128)(2,1)} %field.1, s32[4,2,23]{2,1,0:T(2,128)S(1)} %fusion.count_ref), custom_call_target="tpu_custom_call" | custom-call | tf_op jit(solution)/shard_map/climate/pallas_call | solution.py:509
  48.1 2.9 %anomaly.1 = (bf16[16560,128]{1,0:T(8,128)(2,1)}, bf16[23,2,1440]{2,1,0:T(2,128)(2,1)}) custom-call(s32[4,2,23]{2,1,0:T(2,128)S(1)} %fusion.count_ref, bf16[16560,128]{1,0:T(8,128)(2,1)S(1)} %bitcast.18, f32[4416,128]{1,0:T(8,128)S(1)} %bitcast.17, f32[24,2,11776]{2,1,0:T(2,128)S(1)} %get-tuple-element.7.by_hour), custom_call_target="tpu_custom_call" | custom-call | tf_op jit(solution)/shard_map/anomaly/pallas_call | solution.py:597
  (1 shorter events, 0.0 us)

commit v6 on v5

--- a/solution.py
+++ b/solution.py
@@ -439,6 +439,10 @@
     two.ring.forward()
     one.swap(3)
     two.near()
+    for message in along:
+        message.wait_recv()
+    count2[...] = count1[...] + count_z[0] + count_z[1] + count_z[2]
+    aside = [copy(count2, count_d.at[n], d) for n, d in enumerate(beside)]
     one.swap_first()
     one.late_near()
     two.swap(3)
@@ -447,15 +451,11 @@
     two.swap_first()
     one.late_result()
     two.late_near()
-    for message in along:
-        message.wait_recv()
-    count2[...] = count1[...] + count_z[0] + count_z[1] + count_z[2]
-    aside = [copy(count2, count_d.at[n], d) for n, d in enumerate(beside)]
     one.share_out()
     two.late_ring.forward()
+    windows()
     two.late_result()
     two.share_out()
-    windows()
     one.smooth()
     one.spread_second()
     one.spread_first()

time: 51.2 us -> 51.2 us (level)
  no operation moved by 1% of the time
where the time goes in v6:
time: 51.2 us; the launch traced here: 51 us
  Pallas kernels  49.7 us (97%)
  other arithmetic  0.71 us (1%)
  between operations  0.65 us (1%)
    pallas_call x1, Pallas kernels, climate_of(): pl.pallas_call(reduce_kernel, out_shape=(jax.ShapeDtypeStruct((ROWS, HOUR...  46.8 us
    pallas_call x1, Pallas kernels, anomaly_of(): pl.pallas_call(subtract_kernel, out_shape=(jax.ShapeDtypeStruct((rows, LA...  2.91 us

profile of v6, /device:TPU:0, one launch (start us, length us, event | category | flops | bytes accessed | tf_op | source)
XLA Modules:
  0.0 51.0 jit_solution(3570713788097040165)
XLA Ops:
  0.6 0.7 %fusion.count_ref = s32[4,2,23]{2,1,0:T(2,128)S(1)} fusion(s32[4,23,2]{1,2,0:T(2,128)} %param.5, s32[23]{0:T(128)S(1)} %iota_add_fusion, s32[4,23]{1,0:T(4,128)} %param.4), kind=kLoop, calls=%fused_computation.1 | loop fusion | flops 552 | bytes 1932 | tf_op jit(solution)/shard_map/transpose | solution.py:634
  1.4 46.8 %climate.1 = (f32[24,2,11776]{2,1,0:T(2,128)S(1)}, bf16[4,23,2,11520]{3,2,1,0:T(2,128)(2,1)S(1)}) custom-call(bf16[4,23,2,11520]{3,2,1,0:T(2,128)(2,1)} %field.1, s32[4,2,23]{2,1,0:T(2,128)S(1)} %fusion.count_ref), custom_call_target="tpu_custom_call" | custom-call | tf_op jit(solution)/shard_map/climate/pallas_call | solution.py:509
  48.1 2.9 %anomaly.1 = (bf16[16560,128]{1,0:T(8,128)(2,1)}, bf16[23,2,1440]{2,1,0:T(2,128)(2,1)}) custom-call(s32[4,2,23]{2,1,0:T(2,128)S(1)} %fusion.count_ref, bf16[16560,128]{1,0:T(8,128)(2,1)S(1)} %bitcast.18, f32[4416,128]{1,0:T(8,128)S(1)} %bitcast.17, f32[24,2,11776]{2,1,0:T(2,128)S(1)} %get-tuple-element.7.by_hour), custom_call_target="tpu_custom_call" | custom-call | tf_op jit(solution)/shard_map/anomaly/pallas_call | solution.py:597
  (1 shorter events, 0.0 us)
